TPU v7x, 32 devices: a 4x4x1 block of a 4x4x8 slice. The times are simulated.
32 devices in a mesh: dp: 1 (over z), etp: 4 (over y), ep: 8 (over x, core).
Axes of the slice: x: 4, y: 4, z: 1, core: 2. Of those that a mesh axis runs over, the one named last changes fastest.
The devices are a block of a 4x4x8 slice.
Arguments:
- u_rows: bfloat16 [2048, 1536], P(('dp', 'ep', 'etp'))
- dy_rows: bfloat16 [2048, 1536], P(('dp', 'ep', 'etp'))
- topk_ids: int32 [2048, 4], P(('dp', 'ep', 'etp'))
- w_router: bfloat16 [1536, 32], replicated
- w_gate: bfloat16 [32, 1536, 768], P('ep', None, 'etp')
- w_up: bfloat16 [32, 1536, 768], P('ep', None, 'etp')
- w_down: bfloat16 [32, 768, 1536], P('ep', 'etp')
Outputs:
- output 1: bfloat16 [2048, 1536], P(('dp', 'ep', 'etp'))
- output 2: bfloat16 [2048, 1536], P(('dp', 'ep', 'etp'))
- output 3: float32 [32, 1536, 768], P(('dp', 'ep'), None, 'etp')
- output 4: float32 [32, 1536, 768], P(('dp', 'ep'), None, 'etp')
- output 5: float32 [32, 768, 1536], P(('dp', 'ep'), 'etp')
- output 6: float32 [1536, 32], P('dp')
All inputs are finite; a program needn't handle non-finite values.
Results may differ from a plain program's by a relative error of at most 0.0112773.
Values are sent between devices in bfloat16 or wider.
A program may use at most 768 MiB of HBM per device.

v0:
```python
import jax
import jax.numpy as jnp
from jax import lax
from jax.sharding import PartitionSpec as P


def row_bound(tok_dev, top_k, experts):
    return min(tok_dev, (4 * tok_dev * top_k + experts - 1) // experts)


def slot_layout(expert_ids, experts, slot_count):
    tokens, top_k = expert_ids.shape
    flat_ids = expert_ids.reshape(-1)
    one_hot = (flat_ids[:, None] == jnp.arange(experts, dtype=jnp.int32)[None, :]).astype(jnp.int32)
    pair_rank = jnp.sum((jnp.cumsum(one_hot, axis=0) - one_hot) * one_hot, axis=1)
    pair_slot = flat_ids * slot_count + pair_rank
    slot_pair = jnp.full((experts * slot_count,), tokens * top_k, jnp.int32).at[pair_slot].set(jnp.arange(tokens * top_k, dtype=jnp.int32))
    return pair_slot.reshape(tokens, top_k), slot_pair


def solution(mesh):
    ep_size = mesh.shape["ep"]
    etp_size = mesh.shape["etp"]
    tok_spec = P(("dp", "ep", "etp"), None)
    col_spec = P("ep", None, "etp")
    row_spec = P("ep", "etp", None)
    in_specs = (tok_spec, tok_spec, tok_spec, P(None, None), col_spec, col_spec, row_spec)
    out_specs = (tok_spec, tok_spec, P(("dp", "ep"), None, "etp"), P(("dp", "ep"), None, "etp"), P(("dp", "ep"), "etp", None), P("dp", None))

    def device_step(u_loc, dy_loc, ids_loc, w_router, w_gate, w_up, w_down):
        tok_dev, d_model = u_loc.shape
        top_k = ids_loc.shape[1]
        experts = w_router.shape[1]
        local_exp = w_gate.shape[0]
        cap_slots = etp_size * row_bound(tok_dev, top_k, experts)
        logits = jnp.dot(u_loc, w_router, preferred_element_type=jnp.float32)
        router_prob = jax.nn.softmax(logits, axis=-1)
        gate_loc = jnp.take_along_axis(router_prob, ids_loc, axis=1)
        u_grp = lax.all_gather(u_loc, "etp", axis=0, tiled=True)
        ids_grp = lax.all_gather(ids_loc, "etp", axis=0, tiled=True)
        gate_grp = lax.all_gather(gate_loc, "etp", axis=0, tiled=True)
        pair_slot, slot_pair = slot_layout(ids_grp, experts, cap_slots)
        slot_tok = slot_pair // top_k
        x_send = jnp.take(u_grp, slot_tok, axis=0, mode="fill", fill_value=0)
        x_recv = lax.all_to_all(x_send.reshape(experts, cap_slots, d_model), "ep", 0, 0, tiled=True).reshape(ep_size, local_exp, cap_slots, d_model)
        h_gate = jnp.einsum("secd,edf->secf", x_recv, w_gate, preferred_element_type=jnp.float32).astype(jnp.bfloat16)
        h_up = jnp.einsum("secd,edf->secf", x_recv, w_up, preferred_element_type=jnp.float32).astype(jnp.bfloat16)
        gate_f32 = h_gate.astype(jnp.float32)
        up_f32 = h_up.astype(jnp.float32)
        sig_gate = jax.nn.sigmoid(gate_f32)
        silu_gate = gate_f32 * sig_gate
        act_rows = (silu_gate * up_f32).astype(jnp.bfloat16)
        out_part = jnp.einsum("secf,efd->secd", act_rows, w_down, preferred_element_type=jnp.float32).astype(jnp.bfloat16)
        out_back = lax.all_to_all(out_part.reshape(experts, cap_slots, d_model), "ep", 0, 0, tiled=True)
        out_pairs = jnp.take(out_back.reshape(experts * cap_slots, d_model), pair_slot, axis=0)
        moe_part = jnp.einsum("tk,tkd->td", gate_grp, out_pairs, preferred_element_type=jnp.float32)
        moe_own = lax.psum_scatter(moe_part, "etp", scatter_dimension=0, tiled=True)
        y_loc = (u_loc.astype(jnp.float32) + moe_own).astype(jnp.bfloat16)

        dy_grp = lax.all_gather(dy_loc, "etp", axis=0, tiled=True)
        dgate_part = jnp.einsum("td,tkd->tk", dy_grp, out_pairs, preferred_element_type=jnp.float32)
        dgate_loc = lax.psum_scatter(dgate_part, "etp", scatter_dimension=0, tiled=True)
        slot_gate = jnp.take(gate_grp.reshape(-1), slot_pair, mode="fill", fill_value=0.0)
        cot_slots = jnp.take(dy_grp, slot_tok, axis=0, mode="fill", fill_value=0)
        do_send = (cot_slots.astype(jnp.float32) * slot_gate[:, None]).astype(jnp.bfloat16)
        do_recv = lax.all_to_all(do_send.reshape(experts, cap_slots, d_model), "ep", 0, 0, tiled=True).reshape(ep_size, local_exp, cap_slots, d_model)
        dw_down = jnp.einsum("secf,secd->efd", act_rows, do_recv, preferred_element_type=jnp.float32)
        d_act = jnp.einsum("secd,efd->secf", do_recv, w_down, preferred_element_type=jnp.float32).astype(jnp.bfloat16).astype(jnp.float32)
        d_gate_h = (d_act * up_f32 * sig_gate * (1.0 + gate_f32 * (1.0 - sig_gate))).astype(jnp.bfloat16)
        d_up_h = (d_act * silu_gate).astype(jnp.bfloat16)
        dw_gate = jnp.einsum("secd,secf->edf", x_recv, d_gate_h, preferred_element_type=jnp.float32)
        dw_up = jnp.einsum("secd,secf->edf", x_recv, d_up_h, preferred_element_type=jnp.float32)
        dx_part = (jnp.einsum("secf,edf->secd", d_gate_h, w_gate, preferred_element_type=jnp.float32) + jnp.einsum("secf,edf->secd", d_up_h, w_up, preferred_element_type=jnp.float32)).astype(jnp.bfloat16)
        dx_back = lax.all_to_all(dx_part.reshape(experts, cap_slots, d_model), "ep", 0, 0, tiled=True)
        dx_pairs = jnp.take(dx_back.reshape(experts * cap_slots, d_model), pair_slot, axis=0)
        du_part = jnp.sum(dx_pairs, axis=1, dtype=jnp.float32)
        du_moe = lax.psum_scatter(du_part, "etp", scatter_dimension=0, tiled=True)
        expert_hot = (ids_loc[:, :, None] == jnp.arange(experts, dtype=jnp.int32)[None, None, :]).astype(jnp.float32)
        d_prob = jnp.einsum("tk,tke->te", dgate_loc, expert_hot)
        d_logit = router_prob * (d_prob - jnp.sum(router_prob * d_prob, axis=-1, keepdims=True))
        dw_router = lax.psum(jnp.einsum("td,te->de", u_loc, d_logit, preferred_element_type=jnp.float32), ("etp", "ep"))
        du_router = jnp.einsum("te,de->td", d_logit, w_router, preferred_element_type=jnp.float32)
        du_loc = (dy_loc.astype(jnp.float32) + du_moe + du_router).astype(jnp.bfloat16)
        return y_loc, du_loc, dw_gate, dw_up, dw_down, dw_router

    return jax.shard_map(device_step, mesh=mesh, in_specs=in_specs, out_specs=out_specs, check_vma=False)
```

profile of v0, /device:TPU:97, one launch (start us, length us, event | category | flops | bytes accessed | tf_op | source)
XLA Modules:
  0.0 968.0 jit_solution(10083974800874654925)
XLA Ops:
  7.2 11.7 %all-gather.1 = s32[4,64,4]{1,2,0:T(4,128)S(1)} all-gather(s32[1,64,4]{1,2,0:T(4,128)} %bitcast.169), channel_id=1, replica_groups=mesh['dp'=1,'etp'=4,'ep'=8] {'etp'}, dimensions={0}, use_global_device_ids=true | all-gather | bytes 5120 | tf_op jit(solution)/shard_map/all_gather | solution.py:40
  18.9 0.1 copy.72
  19.1 0.1 eq.42
  19.2 0.1 eq.38
  19.3 0.1 copy.78
  19.4 0.1 mul.57
  19.6 9.0 reduce-window.6
  28.7 0.1 copy.74
  28.9 0.1 broadcast_add_fusion
  29.1 4.3 scatter_custom_fusion
  33.5 0.6 copy-done.13
  34.1 0.6 fusion.64
  34.7 11.4 %all_gather.13 = bf16[256,1536]{1,0:T(8,128)(2,1)S(1)} all-gather(bf16[64,1536]{1,0:T(8,128)(2,1)} %param.11), channel_id=1, replica_groups=mesh['dp'=1,'etp'=4,'ep'=8] {'etp'}, dimensions={0}, use_global_device_ids=true | all-gather | bytes 983040 | tf_op jit(solution)/shard_map/all_gather | solution.py:39
  46.0 19.3 %gather_fusion.2 = bf16[4096,1536]{1,0:T(8,128)(2,1)} fusion(bf16[256,1536]{1,0:T(8,128)(2,1)S(1)} %all_gather.13, s32[4096]{0:T(1024)S(1)} %get-tuple-element.15), kind=kCustom, calls=%fused_computation.clone | custom fusion | bytes 25182208 | tf_op jit(solution)/shard_map/jit(_take)/gather | solution.py:44
  65.3 7.0 broadcast_select_fusion
  72.3 149.4 %all_to_all.20 = bf16[32,128,1536]{2,1,0:T(8,128)(2,1)S(1)} all-to-all(bf16[32,128,1536]{2,1,0:T(8,128)(2,1)S(1)} %bitcast.161), channel_id=1, replica_groups=mesh['dp'=1,'etp'=4,'ep'=8] {'ep'}, dimensions={0} | all-to-all | bytes 25165824 | tf_op jit(solution)/shard_map/all_to_all | solution.py:45
  221.7 4.2 fusion.37
  225.9 0.8 copy-done.1
  226.7 4.2 fusion.32
  231.0 6.5 fusion.8
  237.4 10.7 %copy.81 = bf16[8,4,128,1536]{3,2,1,0:T(8,128)(2,1)} copy(bf16[8,4,128,1536]{3,2,0,1:T(8,128)(2,1)} %fusion.8) | data formatting | bytes 25165824 | tf_op jit(solution)/shard_map/convert_element_type | solution.py:53
  248.2 6.5 all-to-all-start.1
  254.6 0.1 reduce_sum.43
  255.0 0.8 copy.77
  255.7 0.1 copy.82
  255.9 0.1 reshape.206
  256.1 0.8 fusion.74
  256.9 12.0 %all_gather.15 = bf16[256,1536]{1,0:T(8,128)(2,1)S(1)} all-gather(bf16[64,1536]{1,0:T(8,128)(2,1)S(1)} %copy-done.9), channel_id=1, replica_groups=mesh['dp'=1,'etp'=4,'ep'=8] {'etp'}, dimensions={0}, use_global_device_ids=true | all-gather | bytes 983040 | tf_op jit(solution)/shard_map/all_gather | solution.py:60
  268.9 124.3 %all-to-all-done.1 = bf16[32,128,1536]{2,1,0:T(8,128)(2,1)} async-done(((bf16[32,128,1536]{2,1,0:T(8,128)(2,1)}), bf16[32,128,1536]{2,1,0:T(8,128)(2,1)}, u32[]{:S(2)}, u32[]{:S(2)}) %all-to-all-start.1) | async-done | bytes 12582944 | tf_op jit(solution)/shard_map/all_to_all | solution.py:54
  393.2 13.5 %gather_fusion.3 = bf16[1024,1536]{1,0:T(8,128)(2,1)} fusion(bf16[4096,1536]{1,0:T(8,128)(2,1)} %bitcast.20, s32[1024]{0:T(1024)S(1)} %broadcast_clamp_fusion.1), kind=kCustom, calls=%fused_computation.1.clone | custom fusion | bytes 6295552 | tf_op jit(solution)/shard_map/jit(_take)/gather | solution.py:55
  406.6 6.1 reshape.209
  412.8 7.3 fusion.22
  420.2 0.1 copy.88
  420.3 19.3 %gather_fusion.4 = bf16[4096,1536]{1,0:T(8,128)(2,1)} fusion(bf16[256,1536]{1,0:T(8,128)(2,1)S(1)} %all_gather.15, s32[4096]{0:T(1024)S(1)} %copy-done.17), kind=kCustom, calls=%fused_computation.2.clone | custom fusion | bytes 25182208 | tf_op jit(solution)/shard_map/jit(_take)/gather | solution.py:64
  439.6 0.1 reshape.168
  439.7 1.0 fusion.56
  440.9 2.0 gather_fusion.1
  442.9 0.1 reshape.171
  443.1 9.0 all-gather
  452.1 0.1 copy.102
  452.2 0.1 reshape.123
  452.3 16.7 %gather_fusion = f32[4096]{0:T(1024)S(1)} fusion(f32[1024]{0:T(1024)S(1)} %reshape.123, s32[4096]{0:T(1024)S(1)} %copy-done.19), kind=kCustom, calls=%fused_computation.4 | custom fusion | bytes 49152 | tf_op jit(solution)/shard_map/jit(_take)/gather | solution.py:63
  469.1 7.7 multiply_convert_fusion
  476.8 145.7 %all_to_all.21 = bf16[32,128,1536]{2,1,0:T(8,128)(2,1)S(1)} all-to-all(bf16[32,128,1536]{2,1,0:T(8,128)(2,1)S(1)} %bitcast.160), channel_id=1, replica_groups=mesh['dp'=1,'etp'=4,'ep'=8] {'ep'}, dimensions={0} | all-to-all | bytes 25165824 | tf_op jit(solution)/shard_map/all_to_all | solution.py:66
  622.5 7.5 fusion.16
  630.0 12.4 %fusion.26 = f32[4,8,128,1536]{3,2,1,0:T(8,128)} fusion(bf16[8,4,128,192]{2,3,0,1:T(8,128)(2,1)S(1)} %get-tuple-element.13, bf16[4,1536,192]{1,2,0:T(8,128)(2,1)} %param.15), kind=kOutput, calls=%fused_computation.45 | convolution fusion | flops 2415919104 | bytes 29097984 | tf_op jit(solution)/shard_map/secf,edf->secd/dot_general | solution.py:73
  642.3 16.1 %fusion.9 = bf16[8,4,128,1536]{3,2,0,1:T(8,128)(2,1)} fusion(f32[4,8,128,1536]{3,2,1,0:T(8,128)} %fusion.26, bf16[8,4,128,192]{2,3,0,1:T(8,128)(2,1)} %get-tuple-element.12, bf16[4,1536,192]{1,2,0:T(8,128)(2,1)} %param.16), kind=kOutput, calls=%fused_computation.20 | convolution fusion | flops 2428502016 | bytes 41680896 | tf_op jit(solution)/shard_map/secf,edf->secd/dot_general | solution.py:73
  658.4 10.7 %copy.86 = bf16[8,4,128,1536]{3,2,1,0:T(8,128)(2,1)} copy(bf16[8,4,128,1536]{3,2,0,1:T(8,128)(2,1)} %fusion.9) | data formatting | bytes 25165824 | tf_op jit(solution)/shard_map/convert_element_type | solution.py:73
  669.1 6.4 all-to-all-start.3
  675.5 3.8 fusion.23
  679.3 1.2 copy.131
  680.6 0.3 reduce-scatter.6.cloned.1.call-start
  680.9 133.1 %all-to-all-done.3 = bf16[32,128,1536]{2,1,0:T(8,128)(2,1)} async-done(((bf16[32,128,1536]{2,1,0:T(8,128)(2,1)}), bf16[32,128,1536]{2,1,0:T(8,128)(2,1)}, u32[]{:S(2)}, u32[]{:S(2)}) %all-to-all-start.3) | async-done | bytes 12582944 | tf_op jit(solution)/shard_map/all_to_all | solution.py:74
  814.0 13.5 %gather_fusion.5 = bf16[1024,1536]{1,0:T(8,128)(2,1)} fusion(bf16[4096,1536]{1,0:T(8,128)(2,1)} %bitcast.30, s32[1024]{0:T(1024)S(1)} %broadcast_clamp_fusion.1), kind=kCustom, calls=%fused_computation.3.clone | custom fusion | bytes 6295552 | tf_op jit(solution)/shard_map/jit(_take)/gather | solution.py:75
  827.5 6.1 reshape.215
  833.6 7.7 convert_reduce_fusion
  841.4 0.8 convolution_bitcast_fusion.2
  842.4 1.7 add_convert_fusion.1
  844.1 8.6 fusion.10
  852.7 9.2 convolution_bitcast_fusion
  861.9 4.2 convolution_bitcast_fusion.1
  866.1 1.9 fusion.31
  868.1 91.4 %all-reduce.2.cloned.1.call-done = f32[1536,32]{0,1:T(8,128)} async-done(((f32[1536,32]{0,1:T(8,128)}), f32[1536,32]{0,1:T(8,128)}) %all-reduce.2.cloned.1.call-update) | async-done | bytes 196624 | tf_op jit(solution)/shard_map/psum | solution.py:81
  959.4 1.6 copy.133
  (92 shorter events, 1.2 us)
Async XLA Ops:
  7.2 223.8 %copy-start = (bf16[4,192,1536]{2,1,0:T(8,128)(2,1)S(1)}, bf16[4,192,1536]{2,1,0:T(8,128)(2,1)}, u32[]{:S(2)}) copy-start(bf16[4,192,1536]{2,1,0:T(8,128)(2,1)} %param.17) | copy-start | bytes 7077892
  33.4 0.6 copy-start.13
  34.0 31.2 %copy-start.20 = (pred[4096]{0:T(1024)(128)(4,1)}, pred[4096]{0:T(1024)(128)(4,1)S(1)}, u32[]{:S(2)}) copy-start(pred[4096]{0:T(1024)(128)(4,1)S(1)} %compare_and_fusion) | copy-start | bytes 12292
  34.7 30.6 %copy-start.16 = (s32[4096]{0:T(1024)}, s32[4096]{0:T(1024)S(1)}, u32[]{:S(2)}) copy-start(s32[4096]{0:T(1024)S(1)} %get-tuple-element.15) | copy-start | bytes 49156
  72.3 149.4 %copy-start.8 = (bf16[4,1536,192]{1,2,0:T(8,128)(2,1)S(1)}, bf16[4,1536,192]{1,2,0:T(8,128)(2,1)}, u32[]{:S(2)}) copy-start(bf16[4,1536,192]{1,2,0:T(8,128)(2,1)} %param.16) | copy-start | bytes 7077892
  221.7 5.0 copy-start.1
  221.7 5.0 copy-start.7
  226.7 4.2 copy-start.24
  231.0 6.5 copy-start.26
  248.2 7.8 copy-start.22
  248.2 7.9 copy-start.6
  248.2 7.9 copy-start.11
  248.2 8.7 copy-start.9
  248.2 145.0 %all-to-all-start.1 = ((bf16[32,128,1536]{2,1,0:T(8,128)(2,1)}), bf16[32,128,1536]{2,1,0:T(8,128)(2,1)}, u32[]{:S(2)}, u32[]{:S(2)}) async-start(bf16[32,128,1536]{2,1,0:T(8,128)(2,1)} %bitcast.158), calls=%async_computation.1 | async-start | bytes 25165824 | tf_op jit(solution)/shard_map/all_to_all | solution.py:54
  254.6 185.1 %reduce-scatter.8.cloned.1.call-start = ((), (), s32[]{:S(2)}) async-start(), calls=%async_computation.9 | async-start | bytes 163840 | tf_op jit(solution)/shard_map/reduce_scatter | solution.py:62
  406.6 6.1 copy-start.18
  412.8 7.4 copy-start.15
  412.8 7.4 copy-start.23
  412.8 7.5 copy-start.17
  440.9 11.4 %copy-start.19 = (s32[4096]{0:T(1024)S(1)}, s32[4096]{0:T(1024)}, u32[]{:S(2)}) copy-start(s32[4096]{0:T(1024)} %get-tuple-element.14) | copy-start | bytes 49156
  452.3 16.7 %copy-start.14 = (s32[4096]{0:T(1024)S(1)}, s32[4096]{0:T(1024)}, u32[]{:S(2)}) copy-start(s32[4096]{0:T(1024)} %copy-done.13) | copy-start | bytes 49156
  452.3 16.7 %copy-start.21 = (pred[4096]{0:T(1024)(128)(4,1)S(1)}, pred[4096]{0:T(1024)(128)(4,1)}, u32[]{:S(2)}) copy-start(pred[4096]{0:T(1024)(128)(4,1)} %copy-done.20) | copy-start | bytes 12292
  476.8 145.7 %copy-start.25 = (bf16[4,8,128,192]{2,3,1,0:T(8,128)(2,1)S(1)}, bf16[4,8,128,192]{2,3,1,0:T(8,128)(2,1)}, u32[]{:S(2)}) copy-start(bf16[4,8,128,192]{2,3,1,0:T(8,128)(2,1)} %copy-done.24) | copy-start | bytes 4718596
  622.5 7.5 copy-start.2
  630.0 12.4 %copy-start.3 = (bf16[8,4,128,192]{2,3,0,1:T(8,128)(2,1)}, bf16[8,4,128,192]{2,3,0,1:T(8,128)(2,1)S(1)}, u32[]{:S(2)}) copy-start(bf16[8,4,128,192]{2,3,0,1:T(8,128)(2,1)S(1)} %get-tuple-element.13) | copy-start | bytes 4718596
  669.1 144.9 %all-to-all-start.3 = ((bf16[32,128,1536]{2,1,0:T(8,128)(2,1)}), bf16[32,128,1536]{2,1,0:T(8,128)(2,1)}, u32[]{:S(2)}, u32[]{:S(2)}) async-start(bf16[32,128,1536]{2,1,0:T(8,128)(2,1)} %bitcast.159), calls=%async_computation.4 | async-start | bytes 25165824 | tf_op jit(solution)/shard_map/all_to_all | solution.py:74
  675.5 166.9 %reduce-scatter.4.cloned.1.call-start = ((), (), s32[]{:S(2)}) async-start(), calls=%async_computation.7 | async-start | bytes 1966080 | tf_op jit(solution)/shard_map/reduce_scatter | solution.py:57
  680.6 185.5 %reduce-scatter.6.cloned.1.call-start = ((), (), s32[]{:S(2)}) async-start(), calls=%async_computation.8 | async-start | bytes 1966080 | tf_op jit(solution)/shard_map/reduce_scatter | solution.py:77
  841.4 118.1 %all-reduce.2.cloned.1.call-start = ((), (), s32[]{:S(2)}) async-start(), calls=%async_computation.10 | async-start | bytes 393216 | tf_op jit(solution)/shard_map/psum | solution.py:81
  844.1 8.6 copy-start.5
  844.1 17.8 %slice-start = ((s8[12582912]{0:T(1024)(128)(4,1)}), s8[4194304]{0:T(1024)(128)(4,1)S(1)}, s32[]{:S(2)}) async-start(s8[12582912]{0:T(1024)(128)(4,1)} %bitcast.155), calls=%async_computation.11 | async-start | bytes 8388608
  844.1 17.8 %slice-start.1 = ((s8[12582912]{0:T(1024)(128)(4,1)}), s8[4194304]{0:T(1024)(128)(4,1)S(1)}, s32[]{:S(2)}) async-start(s8[12582912]{0:T(1024)(128)(4,1)} %bitcast.155), calls=%async_computation.12 | async-start | bytes 8388608
  852.7 9.2 slice-start.2
  852.7 9.2 copy-start.4
  861.9 4.3 copy-start.10
  861.9 4.2 copy-start.12
Sparse Core Ops, SparseCore 0:
  420.2 14.6 reduce-scatter.7
  680.7 22.7 reduce-scatter.3
  841.5 21.3 reduce-scatter.5
  866.6 92.7 all-reduce.1
where the time goes:
time: 977 us; the launch traced here: 968 us
  waiting for transfers between devices  349 us (36%)
  blocking collectives  339 us (35%)
  local copies, waits for them, and re-layouts  129 us (13%)
  matrix products  88.4 us (9%)
  other arithmetic  34.1 us (3%)
  between operations  14.7 us (2%)
  starting transfers between devices  13.2 us (1%)
    all_to_all x1, blocking collectives, device_step(): lax.all_to_all(x_send.reshape(experts, cap_slots, d_model), 'ep', 0, 0, t...  149 us
    all_to_all x1, blocking collectives, device_step(): lax.all_to_all(do_send.reshape(experts, cap_slots, d_model), 'ep', 0, 0,...  146 us
    all_to_all x1, waiting for transfers between devices, device_step(): lax.all_to_all(dx_part.reshape(experts, cap_slots, d_model), 'ep', 0, 0,...  133 us
    all_to_all x1, waiting for transfers between devices, device_step(): lax.all_to_all(out_part.reshape(experts, cap_slots, d_model), 'ep', 0, 0,...  124 us
    psum x1, waiting for transfers between devices, device_step(): lax.psum(jnp.einsum('td,te->de', u_loc, d_logit, preferred_element_type=j...  91.4 us
    gather x2, local copies, waits for them, and re-layouts, device_step(): jnp.take(out_back.reshape(experts * cap_slots, d_model), pair_slot, axis=0)  19.6 us
    gather x2, local copies, waits for them, and re-layouts, device_step(): jnp.take(dx_back.reshape(experts * cap_slots, d_model), pair_slot, axis=0)  19.6 us
  transfers between devices with their start and end apart: 6, of which 3 were waited for; matrix products, arithmetic and copies ran while one was open for 8% of the time, Pallas kernels for 0%

commit v1 on v0

v1 whole, which is shorter than its diff:
```python
import jax
import jax.numpy as jnp
from jax import lax
from jax.sharding import PartitionSpec as P


def dot_f32(lhs, rhs, contract):
    return lax.dot_general(lhs, rhs, (contract, ((), ())), preferred_element_type=jnp.float32)


def solution(mesh):
    tok_spec = P(("dp", "ep", "etp"), None)
    col_spec = P("ep", None, "etp")
    row_spec = P("ep", "etp", None)
    in_specs = (tok_spec, tok_spec, tok_spec, P(None, None), col_spec, col_spec, row_spec)
    out_specs = (tok_spec, tok_spec, P(("dp", "ep"), None, "etp"), P(("dp", "ep"), None, "etp"), P(("dp", "ep"), "etp", None), P("dp", None))
    axes = ("ep", "etp")

    def device_step(u_loc, dy_loc, ids_loc, w_router, w_gate, w_up, w_down):
        experts = w_router.shape[1]
        local_exp, d_model, width = w_gate.shape
        logits = jnp.dot(u_loc, w_router, preferred_element_type=jnp.float32)
        prob = jax.nn.softmax(logits, axis=-1)
        hot = jnp.any(ids_loc[:, :, None] == jnp.arange(experts, dtype=jnp.int32)[None, None, :], axis=1)
        gate_loc = jnp.where(hot, prob, 0.0)
        u_all = lax.all_gather(u_loc, axes, axis=0, tiled=True)
        dy_all = lax.all_gather(dy_loc, axes, axis=0, tiled=True)
        gate_all = lax.all_gather(gate_loc, axes, axis=0, tiled=True)
        first = lax.axis_index("ep") * local_exp
        gate = lax.dynamic_slice_in_dim(gate_all, first, local_exp, axis=1)
        gate_wide = jnp.repeat(gate, width, axis=1)
        w1 = jnp.swapaxes(w_gate, 1, 2).reshape(local_exp * width, d_model)
        w3 = jnp.swapaxes(w_up, 1, 2).reshape(local_exp * width, d_model)
        w2 = w_down.reshape(local_exp * width, d_model)
        nt = ((1,), (1,))
        nn = ((1,), (0,))
        tn = ((0,), (0,))
        h1 = dot_f32(u_all, w1, nt).astype(jnp.bfloat16).astype(jnp.float32)
        h3 = dot_f32(u_all, w3, nt).astype(jnp.bfloat16).astype(jnp.float32)
        q = dot_f32(dy_all, w2, nt)
        live = gate_wide > 0
        sig = jax.nn.sigmoid(h1)
        silu = h1 * sig
        act = (silu * h3).astype(jnp.bfloat16).astype(jnp.float32)
        act = jnp.where(live, act, 0.0)
        ga = (gate_wide * act).astype(jnp.bfloat16)
        da = jnp.where(live, gate_wide * q, 0.0).astype(jnp.bfloat16).astype(jnp.float32)
        dgate = jnp.sum((act * q).reshape(-1, local_exp, width), axis=2)
        dh1 = jnp.where(live, da * h3 * sig * (1.0 + h1 * (1.0 - sig)), 0.0).astype(jnp.bfloat16)
        dh3 = jnp.where(live, da * silu, 0.0).astype(jnp.bfloat16)
        y_part = dot_f32(ga, w2, nn)
        du_part = dot_f32(dh1, w1, nn) + dot_f32(dh3, w3, nn)
        dw1 = dot_f32(dh1, u_all, tn)
        dw3 = dot_f32(dh3, u_all, tn)
        dw2 = dot_f32(ga, dy_all, tn)
        y_own = lax.psum_scatter(y_part, axes, scatter_dimension=0, tiled=True)
        du_own = lax.psum_scatter(du_part, axes, scatter_dimension=0, tiled=True)
        dg_wide = lax.dynamic_update_slice_in_dim(jnp.zeros_like(gate_all), dgate, first, axis=1)
        dg_loc = lax.psum_scatter(dg_wide, axes, scatter_dimension=0, tiled=True)
        d_logit = prob * (dg_loc - jnp.sum(prob * dg_loc, axis=-1, keepdims=True))
        dw_router = lax.psum(dot_f32(u_loc, d_logit.astype(jnp.bfloat16), tn), axes)
        du_router = dot_f32(d_logit.astype(jnp.bfloat16), w_router, nt)
        y_loc = (u_loc.astype(jnp.float32) + y_own).astype(jnp.bfloat16)
        du_loc = (dy_loc.astype(jnp.float32) + du_own + du_router).astype(jnp.bfloat16)
        unfold = lambda d: jnp.swapaxes(d.reshape(local_exp, width, d_model), 1, 2)
        return y_loc, du_loc, unfold(dw1), unfold(dw3), dw2.reshape(local_exp, width, d_model), dw_router

    return jax.shard_map(device_step, mesh=mesh, in_specs=in_specs, out_specs=out_specs, check_vma=False)
```

time: 977 us -> 500 us (0.51)
  blocking collectives: 339 us -> 33.3 us
  local copies, waits for them, and re-layouts: 129 us -> 4.39 us
  other arithmetic: 34.1 us -> 5.7 us
  starting transfers between devices: 13.2 us -> 0.78 us
    all_to_all x2 -> x0, blocking collectives: 295 us -> none  [the longest x1 149 us: device_step(): lax.all_to_all(x_send.reshape(experts, cap_slots, d_model), 'ep', 0, 0, t...]
    all_to_all x2 -> x0, waiting for transfers between devices: 257 us -> none  [the longest x1 133 us: device_step(): lax.all_to_all(dx_part.reshape(experts, cap_slots, d_model), 'ep', 0, 0,...]
    reduce_scatter x3 -> x2, waiting for transfers between devices: 0.04 us -> 195 us  [the longest x1 97.8 us: device_step(): du_own = lax.psum_scatter(du_part, axes, scatter_dimension=0, tiled=True)]
    gather x12 -> x0, local copies, waits for them, and re-layouts: 96.7 us -> none  [the longest x2 19.6 us: device_step(): jnp.take(out_back.reshape(experts * cap_slots, d_model), pair_slot, axis=0)]
    all_gather x0 -> x2, waiting for transfers between devices: none -> 49.6 us  [the longest x1 35.7 us: device_step(): dy_all = lax.all_gather(dy_loc, axes, axis=0, tiled=True)]
    convert_element_type x2 -> x0, local copies, waits for them, and re-layouts: 21.5 us -> none  [the longest x1 10.7 us: device_step(): jnp.einsum('secf,efd->secd', act_rows, w_down, preferred_element_type=jnp...]
    unnamed x4 -> x7, waiting for transfers between devices: 0.21 us -> 16.6 us
    all_to_all x2 -> x0, starting transfers between devices: 12.8 us -> none  [the longest x1 6.47 us: device_step(): lax.all_to_all(out_part.reshape(experts, cap_slots, d_model), 'ep', 0, 0,...]
  transfers between devices with their start and end apart: 6 -> 6, of which waited for: 3 -> 6; matrix products, arithmetic and copies ran while one was open for 8% -> 14% of each run, Pallas kernels for 0% -> 0%
where the time goes in v1:
time: 500 us
  waiting for transfers between devices  357 us (71%)
  matrix products  84.5 us (17%)
  blocking collectives  33.3 us (7%)
  between operations  14.4 us (3%)
  other arithmetic  5.7 us (1%)
    reduce_scatter x1, waiting for transfers between devices, device_step(): du_own = lax.psum_scatter(du_part, axes, scatter_dimension=0, tiled=True)  97.8 us
    reduce_scatter x1, waiting for transfers between devices, device_step(): y_own = lax.psum_scatter(y_part, axes, scatter_dimension=0, tiled=True)  97.4 us
    psum x1, waiting for transfers between devices, device_step(): dw_router = lax.psum(dot_f32(u_loc, d_logit.astype(jnp.bfloat16), tn), axes)  95.7 us
    dot_general x11, matrix products, dot_f32(): lax.dot_general(lhs, rhs, (contract, ((), ())), preferred_element_type=jn...  83.4 us
    all_gather x1, waiting for transfers between devices, device_step(): dy_all = lax.all_gather(dy_loc, axes, axis=0, tiled=True)  35.7 us
    all_gather x1, blocking collectives, device_step(): gate_all = lax.all_gather(gate_loc, axes, axis=0, tiled=True)  33.3 us
    unnamed x7, waiting for transfers between devices  16.6 us
    all_gather x1, waiting for transfers between devices, device_step(): u_all = lax.all_gather(u_loc, axes, axis=0, tiled=True)  14 us
  transfers between devices with their start and end apart: 6, of which 6 were waited for; matrix products, arithmetic and copies ran while one was open for 14% of the time, Pallas kernels for 0%

profile of v1, /device:TPU:97, one launch (start us, length us, event | category | flops | bytes accessed | tf_op | source)
XLA Modules:
  0.0 500.1 jit_solution(7469473901682972132)
XLA Ops:
  7.2 0.0 copy-start
  7.2 0.1 all-gather.4.cloned.1.call-start
  7.3 0.7 all-gather.4.cloned.1.call-update
  8.0 0.1 all-gather.6.cloned.1.call-start
  8.1 0.7 all-gather.6.cloned.1.call-update
  8.8 0.1 reduce-scatter.10.cloned.1.call-start
  8.9 1.2 fusion.20
  10.1 0.7 fusion.17
  10.8 33.3 %all-gather = f32[32,64,32]{1,2,0:T(8,128)S(1)} all-gather(f32[1,64,32]{1,2,0:T(8,128)S(1)} %select_bitcast_fusion), channel_id=1, replica_groups=mesh['dp'=1,'etp'=4,'ep'=8] {'ep','etp'}, dimensions={0}, use_global_device_ids=true | all-gather | bytes 270336 | tf_op jit(solution)/shard_map/all_gather | solution.py:28
  44.1 0.3 copy.18
  44.4 0.2 reshape.49
  44.6 14.0 %all-gather.4.cloned.1.call-done = bf16[2048,1536]{1,0:T(8,128)(2,1)} async-done(((bf16[64,1536]{1,0:T(8,128)(2,1)}), bf16[2048,1536]{1,0:T(8,128)(2,1)}) %all-gather.4.cloned.1.call-update) | async-done | bytes 6291472 | tf_op jit(solution)/shard_map/all_gather | solution.py:26
  58.6 9.0 %convolution_convert_fusion = bf16[2048,768]{0,1:T(8,128)(2,1)} fusion(bf16[2048,1536]{1,0:T(8,128)(2,1)} %all-gather.4.cloned.1.call-done, bf16[768,1536]{1,0:T(8,128)(2,1)} %bitcast.83), kind=kOutput, calls=%fused_computation.26 | convolution fusion | flops 4833411072 | bytes 11796480 | tf_op jit(solution)/shard_map/dot_general | solution.py:8
  67.6 35.7 %all-gather.6.cloned.1.call-done = bf16[2048,1536]{1,0:T(8,128)(2,1)} async-done(((bf16[64,1536]{1,0:T(8,128)(2,1)}), bf16[2048,1536]{1,0:T(8,128)(2,1)}) %all-gather.6.cloned.1.call-update) | async-done | bytes 6291472 | tf_op jit(solution)/shard_map/all_gather | solution.py:27
  103.3 0.0 copy-start.2
  103.3 0.0 copy-start.6
  103.3 8.0 %fusion.22 = f32[2048,768]{0,1:T(8,128)S(1)} fusion(bf16[2048,1536]{1,0:T(8,128)(2,1)} %all-gather.6.cloned.1.call-done, bf16[768,1536]{1,0:T(8,128)(2,1)} %bitcast.81), kind=kOutput, calls=%fused_computation.44 | convolution fusion | flops 4831838208 | bytes 14942208 | tf_op jit(solution)/shard_map/dot_general | solution.py:8
  111.3 0.0 copy-done
  111.4 0.0 copy-done.2
  111.4 0.0 copy-done.6
  111.4 12.4 %fusion.12 = (bf16[2048,768]{0,1:T(8,128)(2,1)}, f32[2048,768]{0,1:T(8,128)}, bf16[2048,768]{0,1:T(8,128)(2,1)}, bf16[2048,768]{0,1:T(8,128)(2,1)}) fusion(bf16[2048,768]{0,1:T(8,128)(2,1)S(1)} %copy-done.6, f32[2048,4]{0,1:T(4,128)S(1)} %constant_dynamic-slice_fusion, f32[2048,768]{0,1:T(8,128)S(1)} %fusion.22, bf16[2048,1536]{1,0:T(8,128)(2,1)S(1)} %copy-done.2, ...), kind=kOutput, calls=%fused_computation.22 | convolution fusion | flops 4879024128 | bytes 33849344 | tf_op jit(solution)/shard_map/dot_general | solution.py:8
  123.8 3.2 reduce_sum.28
  127.1 1.3 copy.19
  128.4 0.1 reduce-scatter.10.cloned.1.call-update
  128.5 0.2 reduce-scatter.6.cloned.1.call-start
  128.7 10.1 %fusion.21 = f32[2048,1536]{1,0:T(8,128)} fusion(bf16[2048,768]{0,1:T(8,128)(2,1)} %get-tuple-element.9, bf16[768,1536]{1,0:T(8,128)(2,1)} %bitcast.82), kind=kOutput, calls=%fused_computation.43 | convolution fusion | flops 4831838208 | bytes 18087936 | tf_op jit(solution)/shard_map/dot_general | solution.py:8
  138.8 0.1 reduce-scatter.6.cloned.1.call-update
  138.9 0.1 reduce-scatter.8.cloned.1.call-start
  139.0 0.0 copy-start.3
  139.0 0.0 copy-start.10
  139.0 7.2 %fusion.23 = f32[2048,1536]{1,0:T(8,128)S(1)} fusion(bf16[2048,768]{0,1:T(8,128)(2,1)} %get-tuple-element.6, bf16[768,1536]{1,0:T(8,128)(2,1)S(1)} %bitcast.77), kind=kOutput, calls=%fused_computation.45 | convolution fusion | flops 4831838208 | bytes 18087936 | tf_op jit(solution)/shard_map/dot_general | solution.py:8
  146.1 0.0 copy-done.3
  146.2 0.0 copy-done.10
  146.2 8.0 %convolution_add_fusion = f32[2048,1536]{1,0:T(8,128)} fusion(f32[2048,1536]{1,0:T(8,128)S(1)} %fusion.23, bf16[2048,768]{0,1:T(8,128)(2,1)S(1)} %copy-done.3, bf16[768,1536]{1,0:T(8,128)(2,1)S(1)} %bitcast.84), kind=kOutput, calls=%fused_computation.10 | convolution fusion | flops 4834983936 | bytes 30670848 | tf_op jit(solution)/shard_map/dot_general | solution.py:8
  154.1 0.1 reduce-scatter.8.cloned.1.call-update
  154.2 0.3 all-reduce.2.cloned.1.call-start
  154.5 0.0 copy-start.5
  154.5 0.0 slice-start
  154.5 9.6 %fusion.26 = f32[768,1536]{1,0:T(8,128)} fusion(bf16[2048,768]{0,1:T(8,128)(2,1)} %get-tuple-element.9, bf16[2048,1536]{1,0:T(8,128)(2,1)} %all-gather.6.cloned.1.call-done), kind=kOutput, calls=%fused_computation.48 | convolution fusion | flops 4831838208 | bytes 14155776 | tf_op jit(solution)/shard_map/dot_general | solution.py:8
  164.1 0.0 copy-done.5
  164.1 0.0 slice-start.1
  164.1 9.6 %fusion.24 = f32[768,1536]{1,0:T(8,128)} fusion(bf16[2048,768]{0,1:T(8,128)(2,1)S(1)} %copy-done.5, bf16[2048,1536]{1,0:T(8,128)(2,1)} %all-gather.4.cloned.1.call-done), kind=kOutput, calls=%fused_computation.46 | convolution fusion | flops 4831838208 | bytes 14155776 | tf_op jit(solution)/shard_map/dot_general | solution.py:8
  173.7 0.0 slice-done
  173.7 0.0 slice-done.1
  173.7 0.0 copy-done.4
  173.8 0.0 copy-start.7
  173.8 0.0 copy-start.8
  173.8 0.0 copy-start.9
  173.8 0.0 copy-start.1
  173.8 6.7 %fusion.25 = f32[768,1536]{1,0:T(8,128)} fusion(bf16[2048,768]{0,1:T(8,128)(2,1)S(1)} %copy-done.4, bf16[2048,1536]{1,0:T(8,128)(2,1)S(1)} %bitcast.80), kind=kOutput, calls=%fused_computation.47 | convolution fusion | flops 4831838208 | bytes 14155776 | tf_op jit(solution)/shard_map/dot_general | solution.py:8
  180.5 15.0 %reduce-scatter.10.cloned.1.call-done = f32[64,32]{1,0:T(8,128)} async-done(((f32[2048,32]{1,0:T(8,128)}), f32[64,32]{1,0:T(8,128)}) %reduce-scatter.10.cloned.1.call-update) | async-done | bytes 8208
  195.4 0.8 copy.20
  196.3 0.0 copy-done.7
  196.3 0.8 convolution_bitcast_fusion
  197.2 0.1 all-reduce.2.cloned.1.call-update
  197.2 97.4 %reduce-scatter.6.cloned.1.call-done = f32[64,1536]{1,0:T(8,128)} async-done(((f32[2048,1536]{1,0:T(8,128)}), f32[64,1536]{1,0:T(8,128)}) %reduce-scatter.6.cloned.1.call-update) | async-done | bytes 393232 | tf_op jit(solution)/shard_map/reduce_scatter | solution.py:56
  294.6 1.7 add_convert_fusion
  296.3 97.8 %reduce-scatter.8.cloned.1.call-done = f32[64,1536]{1,0:T(8,128)} async-done(((f32[2048,1536]{1,0:T(8,128)}), f32[64,1536]{1,0:T(8,128)}) %reduce-scatter.8.cloned.1.call-update) | async-done | bytes 393232 | tf_op jit(solution)/shard_map/reduce_scatter | solution.py:57
  394.1 0.0 copy-done.8
  394.1 0.0 copy-done.9
  394.1 1.9 fusion.16
  396.0 95.7 %all-reduce.2.cloned.1.call-done = f32[1536,32]{0,1:T(8,128)} async-done(((f32[1536,32]{0,1:T(8,128)}), f32[1536,32]{0,1:T(8,128)}) %all-reduce.2.cloned.1.call-update) | async-done | bytes 196624 | tf_op jit(solution)/shard_map/psum | solution.py:61
  491.6 1.6 copy.23
  493.2 0.0 copy-done.1
  (9 shorter events, 0.1 us)
Async XLA Ops:
  7.2 104.2 %copy-start = (bf16[4,1536,192]{1,2,0:T(8,128)(2,1)S(1)}, bf16[4,1536,192]{1,2,0:T(8,128)(2,1)}, u32[]{:S(2)}) copy-start(bf16[4,1536,192]{1,2,0:T(8,128)(2,1)} %param.11) | copy-start | bytes 7077892
  7.2 51.4 %all-gather.4.cloned.1.call-start = ((), (), s32[]{:S(2)}) async-start(), calls=%async_computation.3 | async-start | bytes 6488064 | tf_op jit(solution)/shard_map/all_gather | solution.py:26
  8.0 95.3 %all-gather.6.cloned.1.call-start = ((), (), s32[]{:S(2)}) async-start(), calls=%async_computation.5 | async-start | bytes 6488064 | tf_op jit(solution)/shard_map/all_gather | solution.py:27
  8.8 186.6 %reduce-scatter.10.cloned.1.call-start = ((), (), s32[]{:S(2)}) async-start(), calls=%async_computation.8 | async-start | bytes 1081344
  103.3 8.1 %copy-start.2 = (bf16[2048,1536]{1,0:T(8,128)(2,1)S(1)}, bf16[2048,1536]{1,0:T(8,128)(2,1)}, u32[]{:S(2)}) copy-start(bf16[2048,1536]{1,0:T(8,128)(2,1)} %all-gather.4.cloned.1.call-done) | copy-start | bytes 18874372
  103.3 8.1 %copy-start.6 = (bf16[2048,768]{0,1:T(8,128)(2,1)S(1)}, bf16[2048,768]{0,1:T(8,128)(2,1)}, u32[]{:S(2)}) copy-start(bf16[2048,768]{0,1:T(8,128)(2,1)} %convolution_convert_fusion) | copy-start | bytes 9437188
  128.5 166.1 %reduce-scatter.6.cloned.1.call-start = ((), (), s32[]{:S(2)}) async-start(), calls=%async_computation.4 | async-start | bytes 12976128 | tf_op jit(solution)/shard_map/reduce_scatter | solution.py:56
  138.9 255.2 %reduce-scatter.8.cloned.1.call-start = ((), (), s32[]{:S(2)}) async-start(), calls=%async_computation.6 | async-start | bytes 12976128 | tf_op jit(solution)/shard_map/reduce_scatter | solution.py:57
  139.0 7.2 %copy-start.3 = (bf16[2048,768]{0,1:T(8,128)(2,1)S(1)}, bf16[2048,768]{0,1:T(8,128)(2,1)}, u32[]{:S(2)}) copy-start(bf16[2048,768]{0,1:T(8,128)(2,1)} %get-tuple-element.8) | copy-start | bytes 9437188
  139.0 7.2 %copy-start.10 = (bf16[4,1536,192]{1,2,0:T(8,128)(2,1)S(1)}, bf16[4,1536,192]{1,2,0:T(8,128)(2,1)}, u32[]{:S(2)}) copy-start(bf16[4,1536,192]{1,2,0:T(8,128)(2,1)} %param.12) | copy-start | bytes 7077892
  154.2 337.5 %all-reduce.2.cloned.1.call-start = ((), (), s32[]{:S(2)}) async-start(), calls=%async_computation.7 | async-start | bytes 393216 | tf_op jit(solution)/shard_map/psum | solution.py:61
  154.5 9.6 %copy-start.5 = (bf16[2048,768]{0,1:T(8,128)(2,1)S(1)}, bf16[2048,768]{0,1:T(8,128)(2,1)}, u32[]{:S(2)}) copy-start(bf16[2048,768]{0,1:T(8,128)(2,1)} %get-tuple-element.6) | copy-start | bytes 9437188
  154.5 19.3 %slice-start = ((s8[6291456]{0:T(1024)(128)(4,1)}), s8[4194304]{0:T(1024)(128)(4,1)S(1)}, s32[]{:S(2)}) async-start(s8[6291456]{0:T(1024)(128)(4,1)} %bitcast.79), calls=%async_computation.9 | async-start | bytes 8388608
  164.1 9.6 %slice-start.1 = ((s8[6291456]{0:T(1024)(128)(4,1)}), s8[2097152]{0:T(1024)(128)(4,1)S(1)}, s32[]{:S(2)}) async-start(s8[6291456]{0:T(1024)(128)(4,1)} %bitcast.79), calls=%async_computation.10 | async-start | bytes 4194304
  164.1 9.6 %copy-start.4 = (bf16[2048,768]{0,1:T(8,128)(2,1)S(1)}, bf16[2048,768]{0,1:T(8,128)(2,1)}, u32[]{:S(2)}) copy-start(bf16[2048,768]{0,1:T(8,128)(2,1)} %get-tuple-element.8) | copy-start | bytes 9437188
  173.8 22.6 %copy-start.7 = (bf16[64,1536]{1,0:T(8,128)(2,1)S(1)}, bf16[64,1536]{1,0:T(8,128)(2,1)}, u32[]{:S(2)}) copy-start(bf16[64,1536]{1,0:T(8,128)(2,1)} %param.7) | copy-start | bytes 589828
  173.8 220.3 %copy-start.8 = (bf16[64,1536]{1,0:T(8,128)(2,1)S(1)}, bf16[64,1536]{1,0:T(8,128)(2,1)}, u32[]{:S(2)}) copy-start(bf16[64,1536]{1,0:T(8,128)(2,1)} %param.8) | copy-start | bytes 589828
  173.8 220.3 %copy-start.9 = (bf16[1536,32]{0,1:T(8,128)(2,1)S(1)}, bf16[1536,32]{0,1:T(8,128)(2,1)}, u32[]{:S(2)}) copy-start(bf16[1536,32]{0,1:T(8,128)(2,1)} %param.10) | copy-start | bytes 294916
  173.8 319.5 %copy-start.1 = (bf16[4,1536,192]{1,2,0:T(8,128)(2,1)S(1)}, bf16[4,1536,192]{1,2,0:T(8,128)(2,1)}, u32[]{:S(2)}) copy-start(bf16[4,1536,192]{1,2,0:T(8,128)(2,1)} %param.11) | copy-start | bytes 7077892
Sparse Core Ops, SparseCore 0:
  10.2 48.4 all-gather.3
  60.7 42.5 all-gather.5
  128.6 66.8 reduce-scatter.9
  199.0 95.5 reduce-scatter.5
  298.1 95.8 reduce-scatter.7
  397.8 93.7 all-reduce.1

commit v2 on v1

--- a/solution.py
+++ b/solution.py
@@ -1,7 +1,276 @@
+import functools
+
 import jax
 import jax.numpy as jnp
 from jax import lax
+from jax.experimental import pallas as pl
+from jax.experimental.pallas import tpu as pltpu
 from jax.sharding import PartitionSpec as P
+
+MESH = pl.DeviceIdType.MESH
+RELS = (2, 1, 3, 0)
+
+
+def wait_all(copies):
+    for copy in copies:
+        copy.wait_send()
+
+
+def reduce_kernel(etp_size, y_hbm, du_hbm, u_hbm, dg_ref, u_ref, dy_ref, wr_ref, prob_ref, y_out, du_out, dwr_out,
+                  mine, peer, relay, inbox, total, stage, relay2, inbox2, u_all, dg_in, dl_in, dl_out,
+                  load_sem, send_sem, recv_sem, dg_send, dg_recv, dl_send, dl_recv):
+    ep_size = mine.shape[1] * 2
+    ring = mine.shape[1]
+    count = ep_size * etp_size
+    ep, etp = lax.axis_index("ep"), lax.axis_index("etp")
+    col, core = ep // 2, ep % 2
+    lin = ep * etp_size + etp
+    tok = u_ref.shape[0]
+    half = tok // 2
+    local_exp = wr_ref.shape[0] // ep_size
+    spots = ((col, etp), (etp, col))
+
+    def at_x(step):
+        return {"ep": lax.rem(col + step + ring, ring) * 2 + core, "etp": etp}
+
+    def at_y(step):
+        return {"ep": ep, "etp": lax.rem(etp + step + etp_size, etp_size)}
+
+    first_axis = (at_x, at_y)
+    second_axis = (at_y, at_x)
+    source = (y_hbm, du_hbm)
+
+    loads = []
+    for rel in RELS:
+        for arr in range(2):
+            pos = lax.rem(spots[arr][0] + rel, ring)
+            src = y_hbm.at[pos, core] if arr == 0 else du_hbm.at[:, core, pos]
+            copy = pltpu.make_async_copy(src, mine.at[arr, pos], load_sem.at[arr, rel])
+            copy.start()
+            loads.append(copy)
+    u_load = pltpu.make_async_copy(u_hbm, u_all, load_sem.at[2, 0])
+    u_load.start()
+
+    barrier = pltpu.get_barrier_semaphore()
+
+    def other(step):
+        dest = lax.rem(lin + step, count)
+        return {"ep": dest // etp_size, "etp": lax.rem(dest, etp_size)}, dest
+
+    def greet(step, carry):
+        pl.semaphore_signal(barrier, inc=1, device_id=other(step)[0], device_id_type=MESH)
+        return carry
+
+    lax.fori_loop(1, count, greet, 0)
+    pl.semaphore_wait(barrier, count - 1)
+
+    def dg_copy(step):
+        device, dest = other(step)
+        return pltpu.make_async_remote_copy(dg_ref.at[dest], dg_in.at[lin], dg_send.at[step], dg_recv.at[lin], device_id=device, device_id_type=MESH)
+
+    def dl_copy(step):
+        device, dest = other(step)
+        return pltpu.make_async_remote_copy(dl_out, dl_in.at[lin], dl_send.at[step], dl_recv.at[lin], device_id=device, device_id_type=MESH)
+
+    def start_dg(step, carry):
+        dg_copy(step).start()
+        return carry
+
+    lax.fori_loop(1, count, start_dg, 0)
+    dg_in[lin] = dg_ref[lin]
+
+    sends = []
+    slots = [0]
+
+    def send(src, dst, device):
+        slot = slots[0]
+        slots[0] += 1
+        copy = pltpu.make_async_remote_copy(src, dst, send_sem.at[slot], recv_sem.at[slot], device_id=device, device_id_type=MESH)
+        copy.start()
+        sends.append(copy)
+        return copy
+
+    partner = {"ep": col * 2 + 1 - core, "etp": etp}
+    swaps = {}
+    for rel in RELS:
+        for arr in range(2):
+            pos = lax.rem(spots[arr][0] + rel, ring)
+            src = y_hbm.at[pos, 1 - core] if arr == 0 else du_hbm.at[:, 1 - core, pos]
+            swaps[arr, rel] = send(src, peer.at[arr, pos], partner)
+
+    def ready(arr, rel):
+        loads[RELS.index(rel) * 2 + arr].wait()
+        swaps[arr, rel].wait_recv()
+
+    def place(arr, rel):
+        return lax.rem(spots[arr][0] + rel, ring)
+
+    def inner(arr, sub):
+        return lax.rem(spots[arr][1] + sub, ring)
+
+    def value(arr, rel, sub):
+        pos, idx = place(arr, rel), inner(arr, sub)
+        return mine[arr, pos, idx].astype(jnp.float32) + peer[arr, pos, idx].astype(jnp.float32)
+
+    def put(arr, rel, sub, val):
+        mine[arr, place(arr, rel), inner(arr, sub)] = val.astype(jnp.bfloat16)
+        return mine.at[arr, place(arr, rel), inner(arr, sub)]
+
+    hops = {}
+    for arr in range(2):
+        ready(arr, 2)
+        for slot, sub, step in ((0, 2, 1), (2, 3, -1), (1, 1, 1), (3, 0, -1)):
+            hops["far", arr, sub] = send(put(arr, 2, sub, value(arr, 2, sub)), relay.at[arr, slot], first_axis[arr](step))
+    for arr in range(2):
+        ready(arr, 1)
+        ready(arr, 3)
+        for sub_r, sub_l in ((3, 2), (0, 1)):
+            hops["left", arr, sub_r] = send(put(arr, 1, sub_r, value(arr, 1, sub_r)), inbox.at[arr, 0, sub_r], first_axis[arr](1))
+            hops["right", arr, sub_l] = send(put(arr, 3, sub_l, value(arr, 3, sub_l)), inbox.at[arr, 1, sub_l], first_axis[arr](-1))
+
+    def wait_dg(step, carry):
+        src = lax.rem(lin + step, count)
+        pltpu.make_async_copy(dg_ref.at[0], dg_in.at[src], dg_recv.at[src]).wait()
+        return carry
+
+    lax.fori_loop(1, count, wait_dg, 0)
+    rows = []
+    for group in range(ep_size):
+        tile = dg_in[group * etp_size]
+        for part in range(1, etp_size):
+            tile = tile + dg_in[group * etp_size + part]
+        rows.append(tile[:local_exp])
+    d_gate = jnp.concatenate(rows, axis=0)
+    prob = prob_ref[...]
+    d_logit = prob * (d_gate - jnp.sum(prob * d_gate, axis=0, keepdims=True))
+    dl_out[...] = d_logit.astype(jnp.bfloat16)
+    dl_in[lin] = d_logit.astype(jnp.bfloat16)
+
+    def start_dl(step, carry):
+        dl_copy(step).start()
+        return carry
+
+    lax.fori_loop(1, count, start_dl, 0)
+
+    for slot_r, sub_r, slot_l, sub_l in ((0, 2, 2, 3), (1, 1, 3, 0)):
+        for arr in range(2):
+            hops["far", arr, sub_r].wait_recv()
+            val = value(arr, 1, sub_r) + relay[arr, slot_r].astype(jnp.float32)
+            hops["left", arr, sub_r] = send(put(arr, 1, sub_r, val), inbox.at[arr, 0, sub_r], first_axis[arr](1))
+            hops["far", arr, sub_l].wait_recv()
+            val = value(arr, 3, sub_l) + relay[arr, slot_l].astype(jnp.float32)
+            hops["right", arr, sub_l] = send(put(arr, 3, sub_l, val), inbox.at[arr, 1, sub_l], first_axis[arr](-1))
+
+    for arr in range(2):
+        ready(arr, 0)
+
+    def settle(arr, sub):
+        hops["left", arr, sub].wait_recv()
+        hops["right", arr, sub].wait_recv()
+        return value(arr, 0, sub) + inbox[arr, 0, sub].astype(jnp.float32) + inbox[arr, 1, sub].astype(jnp.float32)
+
+    def ship(arr, sub, part, val, dst, step):
+        rows_at = pl.ds(part * half, half)
+        stage[arr, sub - 1, rows_at] = val.astype(jnp.bfloat16)
+        return send(stage.at[arr, sub - 1, rows_at], dst, second_axis[arr](step))
+
+    for arr in range(2):
+        val = settle(arr, 2)
+        hops["far2", arr, 0] = ship(arr, 2, 0, val[:half], relay2.at[arr, 0], 1)
+        hops["far2", arr, 1] = ship(arr, 2, 1, val[half:], relay2.at[arr, 1], -1)
+    for arr in range(2):
+        val = settle(arr, 1)
+        hops["left2", arr, 1] = ship(arr, 1, 1, val[half:], inbox2.at[arr, 0, 1], 1)
+        total[arr, 0, :half] = val[:half]
+        val = settle(arr, 3)
+        hops["right2", arr, 0] = ship(arr, 3, 0, val[:half], inbox2.at[arr, 1, 0], -1)
+        total[arr, 0, half:] = val[half:]
+    for arr in range(2):
+        hops["far2", arr, 0].wait_recv()
+        val = total[arr, 0, :half] + relay2[arr, 0].astype(jnp.float32)
+        hops["left2", arr, 0] = ship(arr, 1, 0, val, inbox2.at[arr, 0, 0], 1)
+        hops["far2", arr, 1].wait_recv()
+        val = total[arr, 0, half:] + relay2[arr, 1].astype(jnp.float32)
+        hops["right2", arr, 1] = ship(arr, 3, 1, val, inbox2.at[arr, 1, 1], -1)
+    for arr in range(2):
+        total[arr, 1] = settle(arr, 0)
+
+    def wait_dl(step, carry):
+        src = lax.rem(lin + step, count)
+        pltpu.make_async_copy(dl_out, dl_in.at[src], dl_recv.at[src]).wait()
+        return carry
+
+    lax.fori_loop(1, count, wait_dl, 0)
+    u_load.wait()
+    du_router = lax.dot_general(dl_out[...], wr_ref[...], (((0,), (0,)), ((), ())), preferred_element_type=jnp.float32)[:tok]
+    span = 8
+    dwr_out[...] = jnp.zeros_like(dwr_out)
+
+    def dwr_step(idx, carry):
+        parts = []
+        for pair in range(span // 2):
+            low = dl_in[idx * span + 2 * pair].astype(jnp.float32)
+            high = dl_in[idx * span + 2 * pair + 1].astype(jnp.float32)
+            parts.append((low + pltpu.roll(high, tok, 1)).astype(jnp.bfloat16))
+        lhs = jnp.concatenate(parts, axis=1)
+        rhs = u_all[pl.ds(pl.multiple_of(idx * span * tok, span * tok), span * tok)]
+        dwr_out[...] += jnp.dot(lhs, rhs, preferred_element_type=jnp.float32)
+        return carry
+
+    lax.fori_loop(0, count // span, dwr_step, 0)
+
+    for arr, base, out in ((0, u_ref, y_out), (1, dy_ref, du_out)):
+        for part in range(2):
+            hops["left2", arr, part].wait_recv()
+            hops["right2", arr, part].wait_recv()
+            rows_at = pl.ds(part * half, half)
+            val = base[rows_at].astype(jnp.float32) + total[arr, 1, rows_at] + inbox2[arr, 0, part].astype(jnp.float32) + inbox2[arr, 1, part].astype(jnp.float32)
+            if arr == 1:
+                val = val + du_router[part * half:(part + 1) * half]
+            out[rows_at] = val.astype(jnp.bfloat16)
+    wait_all(sends)
+
+    def drain(step, carry):
+        dg_copy(step).wait_send()
+        dl_copy(step).wait_send()
+        return carry
+
+    lax.fori_loop(1, count, drain, 0)
+
+
+def reduce_call(mesh, y_part, du_part, u_all, dg_tiles, u_loc, dy_loc, wr_t, prob_t):
+    etp_size, ep_size = mesh.shape["etp"], mesh.shape["ep"]
+    tok, d_model = u_loc.shape
+    count, ring, half = etp_size * ep_size, ep_size // 2, tok // 2
+    assert ring == 4 and etp_size == 4
+    shape5 = (ring, 2, etp_size, tok, d_model)
+    vmem = pl.BlockSpec(memory_space=pltpu.VMEM)
+    hbm = pl.BlockSpec(memory_space=pl.ANY)
+    bf16, f32 = jnp.bfloat16, jnp.float32
+    dma = pltpu.SemaphoreType.DMA
+    return pl.pallas_call(
+        functools.partial(reduce_kernel, etp_size),
+        out_shape=(jax.ShapeDtypeStruct((tok, d_model), bf16), jax.ShapeDtypeStruct((tok, d_model), bf16), jax.ShapeDtypeStruct(wr_t.shape, f32)),
+        in_specs=[hbm, hbm, hbm, vmem, vmem, vmem, vmem, vmem],
+        out_specs=(vmem, vmem, vmem),
+        scratch_shapes=[
+            pltpu.VMEM((2, 4, 4, tok, d_model), bf16),
+            pltpu.VMEM((2, 4, 4, tok, d_model), bf16),
+            pltpu.VMEM((2, 4, tok, d_model), bf16),
+            pltpu.VMEM((2, 2, 4, tok, d_model), bf16),
+            pltpu.VMEM((2, 2, tok, d_model), f32),
+            pltpu.VMEM((2, 3, tok, d_model), bf16),
+            pltpu.VMEM((2, 2, half, d_model), bf16),
+            pltpu.VMEM((2, 2, 2, half, d_model), bf16),
+            pltpu.VMEM((count * tok, d_model), bf16),
+            pltpu.VMEM((count, 8, 128), f32),
+            pltpu.VMEM((count, wr_t.shape[0], 128), bf16),
+            pltpu.VMEM((wr_t.shape[0], 128), bf16),
+            dma((3, 4)), dma((48,)), dma((48,)), dma((count,)), dma((count,)), dma((count,)), dma((count,)),
+        ],
+        compiler_params=pltpu.CompilerParams(collective_id=1, has_side_effects=True, vmem_limit_bytes=48 * 1024 * 1024),
+        name="reduce_back",
+    )(y_part.reshape(shape5), du_part.reshape(shape5), u_all, dg_tiles, u_loc, dy_loc, wr_t, prob_t)
 
 
 def dot_f32(lhs, rhs, contract):
@@ -53,15 +322,12 @@
         dw1 = dot_f32(dh1, u_all, tn)
         dw3 = dot_f32(dh3, u_all, tn)
         dw2 = dot_f32(ga, dy_all, tn)
-        y_own = lax.psum_scatter(y_part, axes, scatter_dimension=0, tiled=True)
-        du_own = lax.psum_scatter(du_part, axes, scatter_dimension=0, tiled=True)
-        dg_wide = lax.dynamic_update_slice_in_dim(jnp.zeros_like(gate_all), dgate, first, axis=1)
-        dg_loc = lax.psum_scatter(dg_wide, axes, scatter_dimension=0, tiled=True)
-        d_logit = prob * (dg_loc - jnp.sum(prob * dg_loc, axis=-1, keepdims=True))
-        dw_router = lax.psum(dot_f32(u_loc, d_logit.astype(jnp.bfloat16), tn), axes)
-        du_router = dot_f32(d_logit.astype(jnp.bfloat16), w_router, nt)
-        y_loc = (u_loc.astype(jnp.float32) + y_own).astype(jnp.bfloat16)
-        du_loc = (dy_loc.astype(jnp.float32) + du_own + du_router).astype(jnp.bfloat16)
+        tok, top_k = ids_loc.shape
+        count = u_all.shape[0] // tok
+        dg_tiles = jnp.pad(jnp.swapaxes(dgate.reshape(count, tok, local_exp), 1, 2), ((0, 0), (0, 8 - local_exp), (0, 128 - tok)))
+        prob_t = jnp.pad(prob.T, ((0, 0), (0, 128 - tok)))
+        y_loc, du_loc, dwr_t = reduce_call(mesh, y_part.astype(jnp.bfloat16), du_part.astype(jnp.bfloat16), u_all, dg_tiles, u_loc, dy_loc, w_router.T, prob_t)
+        dw_router = dwr_t.T
         unfold = lambda d: jnp.swapaxes(d.reshape(local_exp, width, d_model), 1, 2)
         return y_loc, du_loc, unfold(dw1), unfold(dw3), dw2.reshape(local_exp, width, d_model), dw_router
 

time: 500 us -> 225 us (0.45)
  waiting for transfers between devices: 357 us -> 44.6 us
  Pallas kernels: 0 us -> 46.1 us
    reduce_scatter x2 -> x0, waiting for transfers between devices: 195 us -> none  [the longest x1 97.8 us: device_step(): du_own = lax.psum_scatter(du_part, axes, scatter_dimension=0, tiled=True)]
    psum x1 -> x0, waiting for transfers between devices: 95.7 us -> none  [device_step(): dw_router = lax.psum(dot_f32(u_loc, d_logit.astype(jnp.bfloat16), tn), axes)]
    pallas_call x0 -> x1, Pallas kernels: none -> 46.1 us  [reduce_call(): pl.pallas_call(functools.partial(reduce_kernel, etp_size), out_shape=(jax...]
    unnamed x7 -> x2, waiting for transfers between devices: 16.6 us -> 1.45 us
    all_gather x1, waiting for transfers between devices: 35.7 us -> 29.1 us  [device_step(): dy_all = lax.all_gather(dy_loc, axes, axis=0, tiled=True)]
    dot_general x11 -> x9, matrix products: 83.4 us -> 79 us  [dot_f32(): lax.dot_general(lhs, rhs, (contract, ((), ())), preferred_element_type=jn...]
  transfers between devices with their start and end apart: 6 -> 2, of which waited for: 6 -> 2; matrix products, arithmetic and copies ran while one was open for 14% -> 8% of each run, Pallas kernels for 0% -> 0%
where the time goes in v2:
time: 225 us
  matrix products  80.1 us (36%)
  Pallas kernels  46.1 us (20%)
  waiting for transfers between devices  44.6 us (20%)
  blocking collectives  33.3 us (15%)
  between operations  14.3 us (6%)
  other arithmetic  3.95 us (2%)
  local copies, waits for them, and re-layouts  2.8 us (1%)
    dot_general x9, matrix products, dot_f32(): lax.dot_general(lhs, rhs, (contract, ((), ())), preferred_element_type=jn...  79 us
    pallas_call x1, Pallas kernels, reduce_call(): pl.pallas_call(functools.partial(reduce_kernel, etp_size), out_shape=(jax...  46.1 us
    all_gather x1, blocking collectives, device_step(): gate_all = lax.all_gather(gate_loc, axes, axis=0, tiled=True)  33.3 us
    all_gather x1, waiting for transfers between devices, device_step(): dy_all = lax.all_gather(dy_loc, axes, axis=0, tiled=True)  29.1 us
    all_gather x1, waiting for transfers between devices, device_step(): u_all = lax.all_gather(u_loc, axes, axis=0, tiled=True)  14 us
  transfers between devices with their start and end apart: 2, of which 2 were waited for; matrix products, arithmetic and copies ran while one was open for 8% of the time, Pallas kernels for 0%

profile of v2, /device:TPU:97, one launch (start us, length us, event | category | flops | bytes accessed | tf_op | source)
XLA Modules:
  0.0 225.2 jit_solution(16257809597168009873)
XLA Ops:
  7.2 0.0 copy-start
  7.2 0.1 all-gather.4.cloned.1.call-start
  7.3 0.7 all-gather.4.cloned.1.call-update
  8.0 0.1 all-gather.6.cloned.1.call-start
  8.1 0.7 all-gather.6.cloned.1.call-update
  8.8 1.2 fusion.20
  10.0 0.7 fusion.16
  10.7 33.3 %all-gather = f32[32,64,32]{1,2,0:T(8,128)S(1)} all-gather(f32[1,64,32]{1,2,0:T(8,128)S(1)} %get-tuple-element.17), channel_id=1, replica_groups=mesh['dp'=1,'etp'=4,'ep'=8] {'ep','etp'}, dimensions={0}, use_global_device_ids=true | all-gather | bytes 270336 | tf_op jit(solution)/shard_map/all_gather | solution.py:297
  44.0 0.3 copy.20
  44.3 0.2 reshape.60
  44.6 14.0 %all-gather.4.cloned.1.call-done.u_hbm = bf16[2048,1536]{1,0:T(8,128)(2,1)} async-done(((bf16[64,1536]{1,0:T(8,128)(2,1)}), bf16[2048,1536]{1,0:T(8,128)(2,1)}) %all-gather.4.cloned.1.call-update) | async-done | bytes 6291472 | tf_op jit(solution)/shard_map/all_gather | solution.py:295
  58.6 0.0 copy-start.5
  58.6 0.0 copy-start.11
  58.6 9.2 %convolution_convert_fusion.1 = bf16[2048,768]{0,1:T(8,128)(2,1)} fusion(bf16[2048,1536]{1,0:T(8,128)(2,1)} %all-gather.4.cloned.1.call-done.u_hbm, bf16[768,1536]{1,0:T(8,128)(2,1)} %bitcast.94), kind=kOutput, calls=%fused_computation.27 | convolution fusion | flops 4833411072 | bytes 11796480 | tf_op jit(solution)/shard_map/dot_general | solution.py:277
  67.8 0.0 copy-done.5
  67.8 0.0 copy-done.11
  67.8 6.4 %convolution_convert_fusion.2 = bf16[2048,768]{0,1:T(8,128)(2,1)} fusion(bf16[2048,1536]{1,0:T(8,128)(2,1)S(1)} %copy-done.5, bf16[768,1536]{1,0:T(8,128)(2,1)S(1)} %bitcast.92), kind=kOutput, calls=%fused_computation.28 | convolution fusion | flops 4833411072 | bytes 11796480 | tf_op jit(solution)/shard_map/dot_general | solution.py:277
  74.2 29.1 %all-gather.6.cloned.1.call-done = bf16[2048,1536]{1,0:T(8,128)(2,1)} async-done(((bf16[64,1536]{1,0:T(8,128)(2,1)}), bf16[2048,1536]{1,0:T(8,128)(2,1)}) %all-gather.6.cloned.1.call-update) | async-done | bytes 6291472 | tf_op jit(solution)/shard_map/all_gather | solution.py:296
  103.3 0.0 copy-done
  103.3 0.0 copy-start.12
  103.3 14.2 %fusion.15 = (f32[2048,768]{0,1:T(8,128)}, bf16[2048,768]{0,1:T(8,128)(2,1)S(1)}, bf16[2048,768]{0,1:T(8,128)(2,1)}, bf16[2048,768]{0,1:T(8,128)(2,1)S(1)}) fusion(f32[2048,4]{0,1:T(4,128)S(1)} %constant_dynamic-slice_fusion, bf16[2048,768]{0,1:T(8,128)(2,1)} %convolution_convert_fusion.1, bf16[2048,768]{0,1:T(8,128)(2,1)} %convolution_convert_fusion.2, ...), kind=kOutput, calls=%fused_computation.26 | convolution fusion | flops 4877451264 | bytes 30703616 | tf_op jit(solution)/shard_map/dot_general | solution.py:277
  117.5 0.0 copy-start.9
  117.5 0.0 copy-start.6
  117.5 0.0 copy-done.12
  117.5 8.0 %fusion.21 = f32[2048,1536]{1,0:T(8,128)} fusion(bf16[2048,768]{0,1:T(8,128)(2,1)S(1)} %get-tuple-element.13, bf16[768,1536]{1,0:T(8,128)(2,1)S(1)} %bitcast.93), kind=kOutput, calls=%fused_computation.39 | convolution fusion | flops 4831838208 | bytes 18087936 | tf_op jit(solution)/shard_map/dot_general | solution.py:277
  125.6 0.0 copy-done.9
  125.6 0.0 copy-done.6
  125.6 7.1 %convolution_convert_fusion = bf16[2048,1536]{1,0:T(8,128)(2,1)} fusion(bf16[2048,768]{0,1:T(8,128)(2,1)S(1)} %get-tuple-element.15, bf16[768,1536]{1,0:T(8,128)(2,1)S(1)} %bitcast.80), kind=kOutput, calls=%fused_computation.14 | convolution fusion | flops 4834983936 | bytes 11796480 | tf_op jit(solution)/shard_map/dot_general | solution.py:277
  132.7 3.2 %reduce_sum.19 = f32[2048,4]{0,1:T(4,128)S(1)} reduce(f32[2048,4,192]{0,2,1:T(8,128)} %bitcast.84, f32[]{:T(128)} %constant.10.clone.1), dimensions={2}, to_apply=%region_3.4 | reduce | flops 1564672 | bytes 6324228 | tf_op jit(solution)/shard_map/reduce_sum | solution.py:317
  135.9 0.1 reshape.55
  136.1 0.0 copy-start.2
  136.1 0.0 copy-start.3
  136.1 0.0 copy-start.4
  136.1 11.1 %add_convert_fusion = bf16[2048,1536]{1,0:T(8,128)(2,1)} fusion(f32[2048,1536]{1,0:T(8,128)} %fusion.21, bf16[2048,768]{0,1:T(8,128)(2,1)} %get-tuple-element.14, bf16[768,1536]{1,0:T(8,128)(2,1)} %bitcast.95), kind=kOutput, calls=%fused_computation.3 | convolution fusion | flops 4838129664 | bytes 24379392 | tf_op jit(solution)/shard_map/dot_general | solution.py:277
  147.2 0.0 copy-done.2
  147.2 0.0 copy-done.3
  147.2 0.0 copy-done.4
  147.2 0.0 copy-start.10
  147.2 0.0 slice-start
  147.2 46.1 %reduce_back.1 = (bf16[64,1536]{1,0:T(8,128)(2,1)S(1)}, bf16[64,1536]{1,0:T(8,128)(2,1)S(1)}, f32[32,1536]{1,0:T(8,128)S(1)}) custom-call(bf16[4,2,4,64,1536]{4,3,2,1,0:T(8,128)(2,1)} %bitcast.89, bf16[4,2,4,64,1536]{4,3,2,1,0:T(8,128)(2,1)} %bitcast.90, bf16[2048,1536]{1,0:T(8,128)(2,1)} %all-gather.4.cloned.1.call-done.u_hbm, ...), custom_call_target="tpu_custom_call" | custom-call | tf_op jit(solution)/shard_map/reduce_back/pallas_call | solution.py:251
  193.3 0.0 copy-done.10
  193.3 0.0 slice-start.1
  193.3 0.0 copy-start.8
  193.4 0.0 slice-start.2
  193.4 9.6 %fusion.22 = f32[768,1536]{1,0:T(8,128)} fusion(bf16[2048,768]{0,1:T(8,128)(2,1)S(1)} %copy-done.10, bf16[2048,1536]{1,0:T(8,128)(2,1)} %all-gather.4.cloned.1.call-done.u_hbm), kind=kOutput, calls=%fused_computation.40 | convolution fusion | flops 4831838208 | bytes 14155776 | tf_op jit(solution)/shard_map/dot_general | solution.py:277
  202.9 0.0 slice-done
  202.9 0.0 slice-done.1
  202.9 0.0 copy-done.8
  202.9 0.0 slice-start.3
  203.0 0.0 copy-start.7
  203.0 6.7 %fusion.23 = f32[768,1536]{1,0:T(8,128)} fusion(bf16[2048,768]{0,1:T(8,128)(2,1)S(1)} %copy-done.8, bf16[2048,1536]{1,0:T(8,128)(2,1)S(1)} %bitcast.86), kind=kOutput, calls=%fused_computation.41 | convolution fusion | flops 4831838208 | bytes 14155776 | tf_op jit(solution)/shard_map/dot_general | solution.py:277
  209.6 0.0 slice-done.2
  209.6 0.0 slice-done.3
  209.6 0.0 copy-done.7
  209.7 0.0 copy-start.1
  209.7 6.7 %fusion.24 = f32[768,1536]{1,0:T(8,128)} fusion(bf16[2048,768]{0,1:T(8,128)(2,1)S(1)} %copy-done.7, bf16[2048,1536]{1,0:T(8,128)(2,1)S(1)} %bitcast.88), kind=kOutput, calls=%fused_computation.42 | convolution fusion | flops 4831838208 | bytes 14155776 | tf_op jit(solution)/shard_map/dot_general | solution.py:277
  216.3 0.7 copy.27
  217.0 0.7 copy.28
  217.7 0.7 copy.29
  218.4 0.0 copy-done.1
  (8 shorter events, 0.1 us)
Async XLA Ops:
  7.2 96.1 %copy-start = (bf16[4,192,1536]{2,1,0:T(8,128)(2,1)S(1)}, bf16[4,192,1536]{2,1,0:T(8,128)(2,1)}, u32[]{:S(2)}) copy-start(bf16[4,192,1536]{2,1,0:T(8,128)(2,1)} %param.13) | copy-start | bytes 7077892
  7.2 51.4 %all-gather.4.cloned.1.call-start = ((), (), s32[]{:S(2)}) async-start(), calls=%async_computation | async-start | bytes 6488064 | tf_op jit(solution)/shard_map/all_gather | solution.py:295
  8.0 95.3 %all-gather.6.cloned.1.call-start = ((), (), s32[]{:S(2)}) async-start(), calls=%async_computation.1 | async-start | bytes 6488064 | tf_op jit(solution)/shard_map/all_gather | solution.py:296
  58.6 9.2 %copy-start.5 = (bf16[2048,1536]{1,0:T(8,128)(2,1)S(1)}, bf16[2048,1536]{1,0:T(8,128)(2,1)}, u32[]{:S(2)}) copy-start(bf16[2048,1536]{1,0:T(8,128)(2,1)} %all-gather.4.cloned.1.call-done.u_hbm) | copy-start | bytes 18874372
  58.6 9.2 %copy-start.11 = (bf16[4,1536,192]{1,2,0:T(8,128)(2,1)S(1)}, bf16[4,1536,192]{1,2,0:T(8,128)(2,1)}, u32[]{:S(2)}) copy-start(bf16[4,1536,192]{1,2,0:T(8,128)(2,1)} %param.11) | copy-start | bytes 7077892
  103.3 14.2 %copy-start.12 = (bf16[4,1536,192]{1,2,0:T(8,128)(2,1)S(1)}, bf16[4,1536,192]{1,2,0:T(8,128)(2,1)}, u32[]{:S(2)}) copy-start(bf16[4,1536,192]{1,2,0:T(8,128)(2,1)} %param.11) | copy-start | bytes 7077892
  117.5 8.0 %copy-start.9 = (bf16[2048,768]{0,1:T(8,128)(2,1)}, bf16[2048,768]{0,1:T(8,128)(2,1)S(1)}, u32[]{:S(2)}) copy-start(bf16[2048,768]{0,1:T(8,128)(2,1)S(1)} %get-tuple-element.13) | copy-start | bytes 9437188
  117.5 8.0 %copy-start.6 = (bf16[2048,768]{0,1:T(8,128)(2,1)}, bf16[2048,768]{0,1:T(8,128)(2,1)S(1)}, u32[]{:S(2)}) copy-start(bf16[2048,768]{0,1:T(8,128)(2,1)S(1)} %get-tuple-element.15) | copy-start | bytes 9437188
  136.1 11.1 %copy-start.2 = (bf16[64,1536]{1,0:T(8,128)(2,1)S(1)}, bf16[64,1536]{1,0:T(8,128)(2,1)}, u32[]{:S(2)}) copy-start(bf16[64,1536]{1,0:T(8,128)(2,1)} %u_ref.1) | copy-start | bytes 589828
  136.1 11.1 %copy-start.3 = (bf16[64,1536]{1,0:T(8,128)(2,1)S(1)}, bf16[64,1536]{1,0:T(8,128)(2,1)}, u32[]{:S(2)}) copy-start(bf16[64,1536]{1,0:T(8,128)(2,1)} %dy_ref.1) | copy-start | bytes 589828
  136.1 11.1 %copy-start.4 = (bf16[1536,32]{0,1:T(8,128)(2,1)S(1)}, bf16[1536,32]{0,1:T(8,128)(2,1)}, u32[]{:S(2)}) copy-start(bf16[1536,32]{0,1:T(8,128)(2,1)} %param.10) | copy-start | bytes 294916
  147.2 46.1 %copy-start.10 = (bf16[2048,768]{0,1:T(8,128)(2,1)S(1)}, bf16[2048,768]{0,1:T(8,128)(2,1)}, u32[]{:S(2)}) copy-start(bf16[2048,768]{0,1:T(8,128)(2,1)} %copy-done.9) | copy-start | bytes 9437188
  147.2 55.7 %slice-start = ((s8[6291456]{0:T(1024)(128)(4,1)}), s8[4194304]{0:T(1024)(128)(4,1)S(1)}, s32[]{:S(2)}) async-start(s8[6291456]{0:T(1024)(128)(4,1)} %bitcast.85), calls=%async_computation.2 | async-start | bytes 8388608
  193.3 9.6 %slice-start.1 = ((s8[6291456]{0:T(1024)(128)(4,1)}), s8[2097152]{0:T(1024)(128)(4,1)S(1)}, s32[]{:S(2)}) async-start(s8[6291456]{0:T(1024)(128)(4,1)} %bitcast.85), calls=%async_computation.3 | async-start | bytes 4194304
  193.3 9.6 %copy-start.8 = (bf16[2048,768]{0,1:T(8,128)(2,1)S(1)}, bf16[2048,768]{0,1:T(8,128)(2,1)}, u32[]{:S(2)}) copy-start(bf16[2048,768]{0,1:T(8,128)(2,1)} %get-tuple-element.14) | copy-start | bytes 9437188
  193.4 16.3 %slice-start.2 = ((s8[6291456]{0:T(1024)(128)(4,1)}), s8[4194304]{0:T(1024)(128)(4,1)S(1)}, s32[]{:S(2)}) async-start(s8[6291456]{0:T(1024)(128)(4,1)} %bitcast.87), calls=%async_computation.4 | async-start | bytes 8388608
  202.9 6.7 %slice-start.3 = ((s8[6291456]{0:T(1024)(128)(4,1)}), s8[2097152]{0:T(1024)(128)(4,1)S(1)}, s32[]{:S(2)}) async-start(s8[6291456]{0:T(1024)(128)(4,1)} %bitcast.87), calls=%async_computation.5 | async-start | bytes 4194304
  203.0 6.7 %copy-start.7 = (bf16[2048,768]{0,1:T(8,128)(2,1)S(1)}, bf16[2048,768]{0,1:T(8,128)(2,1)}, u32[]{:S(2)}) copy-start(bf16[2048,768]{0,1:T(8,128)(2,1)} %copy-done.6) | copy-start | bytes 9437188
  209.7 8.7 %copy-start.1 = (bf16[4,192,1536]{2,1,0:T(8,128)(2,1)S(1)}, bf16[4,192,1536]{2,1,0:T(8,128)(2,1)}, u32[]{:S(2)}) copy-start(bf16[4,192,1536]{2,1,0:T(8,128)(2,1)} %param.13) | copy-start | bytes 7077892
Sparse Core Ops, SparseCore 0:
  10.2 48.4 all-gather.3
  60.7 42.5 all-gather.5

commit v3 on v2

v3 whole, which is shorter than its diff:
```python
import functools

import jax
import jax.numpy as jnp
from jax import lax
from jax.experimental import pallas as pl
from jax.experimental.pallas import tpu as pltpu
from jax.sharding import PartitionSpec as P

MESH = pl.DeviceIdType.MESH
PAIR = range(2)


def each_other(count, step):
    lax.fori_loop(1, count, step, 0)


RELS = (2, 1, 3, 0)


def wait_all(copies):
    for copy in copies:
        copy.wait_send()


def reduce_kernel(etp_size, y_hbm, du_hbm, all_hbm, act_hbm, dg_ref, u_ref, dy_ref, wr_ref, prob_ref, y_out, du_out, dwr_out, dw1_hbm, dw3_hbm, dw2_hbm,
                  mine, peer, relay, inbox, total, stage, relay2, inbox2, all_rows, acts, dw_buf, dg_in, dl_in, dl_out,
                  load_sem, act_sem, dw_sem, send_sem, recv_sem, dg_send, dg_recv, dl_send, dl_recv):
    ep_size = mine.shape[1] * 2
    ring = mine.shape[1]
    count = ep_size * etp_size
    ep, etp = lax.axis_index("ep"), lax.axis_index("etp")
    col, core = ep // 2, ep % 2
    lin = ep * etp_size + etp
    tok = u_ref.shape[0]
    half = tok // 2
    local_exp = wr_ref.shape[0] // ep_size
    spots = ((col, etp), (etp, col))

    def at_x(step):
        return {"ep": lax.rem(col + step + ring, ring) * 2 + core, "etp": etp}

    def at_y(step):
        return {"ep": ep, "etp": lax.rem(etp + step + etp_size, etp_size)}

    first_axis = (at_x, at_y)
    second_axis = (at_y, at_x)
    source = (y_hbm, du_hbm)

    loads = []
    for rel in RELS:
        for arr in PAIR:
            pos = lax.rem(spots[arr][0] + rel, ring)
            src = y_hbm.at[pos, core] if arr == 0 else du_hbm.at[:, core, pos]
            copy = pltpu.make_async_copy(src, mine.at[arr, pos], load_sem.at[arr, rel])
            copy.start()
            loads.append(copy)
    row_loads = [pltpu.make_async_copy(all_hbm.at[arr], all_rows.at[arr], load_sem.at[2, arr]) for arr in PAIR]
    act_loads = [pltpu.make_async_copy(act_hbm.at[kind], acts.at[kind], act_sem.at[kind]) for kind in range(3)]
    for copy in (row_loads[0], act_loads[0], act_loads[1], row_loads[1], act_loads[2]):
        copy.start()

    barrier = pltpu.get_barrier_semaphore()

    def other(step):
        dest = lax.rem(lin + step, count)
        return {"ep": dest // etp_size, "etp": lax.rem(dest, etp_size)}, dest

    def greet(step, carry):
        pl.semaphore_signal(barrier, inc=1, device_id=other(step)[0], device_id_type=MESH)
        return carry

    each_other(count, greet)
    pl.semaphore_wait(barrier, count - 1)

    def dg_copy(step):
        device, dest = other(step)
        return pltpu.make_async_remote_copy(dg_ref.at[dest], dg_in.at[lin], dg_send.at[step], dg_recv.at[lin], device_id=device, device_id_type=MESH)

    def dl_copy(step):
        device, dest = other(step)
        return pltpu.make_async_remote_copy(dl_out, dl_in.at[lin], dl_send.at[step], dl_recv.at[lin], device_id=device, device_id_type=MESH)

    def start_dg(step, carry):
        dg_copy(step).start()
        return carry

    each_other(count, start_dg)
    dg_in[lin] = dg_ref[lin]

    dw_outs = (dw1_hbm, dw3_hbm, dw2_hbm)
    inner, d_model = dw1_hbm.shape
    chunk = 256
    chunks = inner // chunk
    pending = {}

    def dw_step(index):
        kind, part = divmod(index, chunks)
        if part == 0:
            act_loads[kind].wait()
            if kind != 1:
                row_loads[kind // 2].wait()
        slot = index % 2
        if slot in pending:
            pending[slot].wait()
        lhs = acts[kind, :, part * chunk:(part + 1) * chunk]
        dw_buf[slot] = lax.dot_general(lhs, all_rows[kind // 2], (((0,), (0,)), ((), ())), preferred_element_type=jnp.float32)
        pending[slot] = pltpu.make_async_copy(dw_buf.at[slot], dw_outs[kind].at[pl.ds(part * chunk, chunk)], dw_sem.at[slot])
        pending[slot].start()

    sends = []
    slots = [0]

    def send(src, dst, device):
        slot = slots[0]
        slots[0] += 1
        copy = pltpu.make_async_remote_copy(src, dst, send_sem.at[slot], recv_sem.at[slot], device_id=device, device_id_type=MESH)
        copy.start()
        sends.append(copy)
        return copy

    partner = {"ep": col * 2 + 1 - core, "etp": etp}
    swaps = {}
    for rel in RELS:
        for arr in PAIR:
            pos = lax.rem(spots[arr][0] + rel, ring)
            src = y_hbm.at[pos, 1 - core] if arr == 0 else du_hbm.at[:, 1 - core, pos]
            swaps[arr, rel] = send(src, peer.at[arr, pos], partner)

    def ready(arr, rel):
        loads[RELS.index(rel) * 2 + arr].wait()
        swaps[arr, rel].wait_recv()

    def place(arr, rel):
        return lax.rem(spots[arr][0] + rel, ring)

    def inner(arr, sub):
        return lax.rem(spots[arr][1] + sub, ring)

    def value(arr, rel, sub):
        pos, idx = place(arr, rel), inner(arr, sub)
        return mine[arr, pos, idx].astype(jnp.float32) + peer[arr, pos, idx].astype(jnp.float32)

    def put(arr, rel, sub, val):
        mine[arr, place(arr, rel), inner(arr, sub)] = val.astype(jnp.bfloat16)
        return mine.at[arr, place(arr, rel), inner(arr, sub)]

    hops = {}
    for arr in PAIR:
        ready(arr, 2)
        for slot, sub, step in ((0, 2, 1), (2, 3, -1), (1, 1, 1), (3, 0, -1)):
            hops["far", arr, sub] = send(put(arr, 2, sub, value(arr, 2, sub)), relay.at[arr, slot], first_axis[arr](step))
    for arr in PAIR:
        ready(arr, 1)
        ready(arr, 3)
        for sub_r, sub_l in ((3, 2), (0, 1)):
            hops["left", arr, sub_r] = send(put(arr, 1, sub_r, value(arr, 1, sub_r)), inbox.at[arr, 0, sub_r], first_axis[arr](1))
            hops["right", arr, sub_l] = send(put(arr, 3, sub_l, value(arr, 3, sub_l)), inbox.at[arr, 1, sub_l], first_axis[arr](-1))

    for index in range(3):
        dw_step(index)

    def wait_dg(step, carry):
        src = lax.rem(lin + step, count)
        pltpu.make_async_copy(dg_ref.at[0], dg_in.at[src], dg_recv.at[src]).wait()
        return carry

    each_other(count, wait_dg)
    rows = []
    for group in range(ep_size):
        tile = dg_in[group * etp_size]
        for part in range(1, etp_size):
            tile = tile + dg_in[group * etp_size + part]
        rows.append(tile[:local_exp])
    d_gate = jnp.concatenate(rows, axis=0)
    prob = prob_ref[...]
    d_logit = prob * (d_gate - jnp.sum(prob * d_gate, axis=0, keepdims=True))
    dl_out[...] = d_logit.astype(jnp.bfloat16)
    dl_in[lin] = d_logit.astype(jnp.bfloat16)

    def start_dl(step, carry):
        dl_copy(step).start()
        return carry

    each_other(count, start_dl)

    for slot_r, sub_r, slot_l, sub_l in ((0, 2, 2, 3), (1, 1, 3, 0)):
        for index in range(3 + slot_r * 2, 5 + slot_r * 2):
            dw_step(index)
        for arr in PAIR:
            hops["far", arr, sub_r].wait_recv()
            val = value(arr, 1, sub_r) + relay[arr, slot_r].astype(jnp.float32)
            hops["left", arr, sub_r] = send(put(arr, 1, sub_r, val), inbox.at[arr, 0, sub_r], first_axis[arr](1))
            hops["far", arr, sub_l].wait_recv()
            val = value(arr, 3, sub_l) + relay[arr, slot_l].astype(jnp.float32)
            hops["right", arr, sub_l] = send(put(arr, 3, sub_l, val), inbox.at[arr, 1, sub_l], first_axis[arr](-1))

    for arr in PAIR:
        ready(arr, 0)
    for index in range(7, 9):
        dw_step(index)

    def settle(arr, sub):
        hops["left", arr, sub].wait_recv()
        hops["right", arr, sub].wait_recv()
        return value(arr, 0, sub) + inbox[arr, 0, sub].astype(jnp.float32) + inbox[arr, 1, sub].astype(jnp.float32)

    def ship(arr, sub, part, val, dst, step):
        rows_at = pl.ds(part * half, half)
        stage[arr, sub - 1, rows_at] = val.astype(jnp.bfloat16)
        return send(stage.at[arr, sub - 1, rows_at], dst, second_axis[arr](step))

    for arr in PAIR:
        val = settle(arr, 2)
        hops["far2", arr, 0] = ship(arr, 2, 0, val[:half], relay2.at[arr, 0], 1)
        hops["far2", arr, 1] = ship(arr, 2, 1, val[half:], relay2.at[arr, 1], -1)
    for arr in PAIR:
        val = settle(arr, 1)
        hops["left2", arr, 1] = ship(arr, 1, 1, val[half:], inbox2.at[arr, 0, 1], 1)
        total[arr, 0, :half] = val[:half]
        val = settle(arr, 3)
        hops["right2", arr, 0] = ship(arr, 3, 0, val[:half], inbox2.at[arr, 1, 0], -1)
        total[arr, 0, half:] = val[half:]
    for arr in PAIR:
        hops["far2", arr, 0].wait_recv()
        val = total[arr, 0, :half] + relay2[arr, 0].astype(jnp.float32)
        hops["left2", arr, 0] = ship(arr, 1, 0, val, inbox2.at[arr, 0, 0], 1)
        hops["far2", arr, 1].wait_recv()
        val = total[arr, 0, half:] + relay2[arr, 1].astype(jnp.float32)
        hops["right2", arr, 1] = ship(arr, 3, 1, val, inbox2.at[arr, 1, 1], -1)
    for arr in PAIR:
        total[arr, 1] = settle(arr, 0)

    def wait_dl(step, carry):
        src = lax.rem(lin + step, count)
        pltpu.make_async_copy(dl_out, dl_in.at[src], dl_recv.at[src]).wait()
        return carry

    each_other(count, wait_dl)
    du_router = lax.dot_general(dl_out[...], wr_ref[...], (((0,), (0,)), ((), ())), preferred_element_type=jnp.float32)[:tok]
    span = 8
    dwr_out[...] = jnp.zeros_like(dwr_out)

    def dwr_step(idx, carry):
        parts = []
        for pair in range(span // 2):
            low = dl_in[idx * 2 * etp_size + pair].astype(jnp.float32)
            high = dl_in[(idx * 2 + 1) * etp_size + pair].astype(jnp.float32)
            parts.append((low + pltpu.roll(high, tok, 1)).astype(jnp.bfloat16))
        lhs = jnp.concatenate(parts, axis=1)
        rhs = all_rows[0, pl.ds(pl.multiple_of(idx * span * tok, span * tok), span * tok)]
        dwr_out[...] += jnp.dot(lhs, rhs, preferred_element_type=jnp.float32)
        return carry

    lax.fori_loop(0, count // span, dwr_step, 0)

    for arr, base, out in ((0, u_ref, y_out), (1, dy_ref, du_out)):
        for part in PAIR:
            hops["left2", arr, part].wait_recv()
            hops["right2", arr, part].wait_recv()
            rows_at = pl.ds(part * half, half)
            val = base[rows_at].astype(jnp.float32) + total[arr, 1, rows_at] + inbox2[arr, 0, part].astype(jnp.float32) + inbox2[arr, 1, part].astype(jnp.float32)
            if arr == 1:
                val = val + du_router[part * half:(part + 1) * half]
            out[rows_at] = val.astype(jnp.bfloat16)
    wait_all(sends)
    for copy in pending.values():
        copy.wait()

    def drain(step, carry):
        dg_copy(step).wait_send()
        dl_copy(step).wait_send()
        return carry

    each_other(count, drain)


def reduce_call(mesh, y_part, du_part, all_rows, acts, dg_tiles, u_loc, dy_loc, wr_t, prob_t):
    etp_size, ep_size = mesh.shape["etp"], mesh.shape["ep"]
    tok, d_model = u_loc.shape
    count, ring, half = etp_size * ep_size, ep_size // 2, tok // 2
    assert ring == 4 and etp_size == 4
    shape5 = (ring, 2, etp_size, tok, d_model)
    vmem = pl.BlockSpec(memory_space=pltpu.VMEM)
    hbm = pl.BlockSpec(memory_space=pl.ANY)
    bf16, f32 = jnp.bfloat16, jnp.float32
    dma = pltpu.SemaphoreType.DMA
    return pl.pallas_call(
        functools.partial(reduce_kernel, etp_size),
        out_shape=(jax.ShapeDtypeStruct((tok, d_model), bf16), jax.ShapeDtypeStruct((tok, d_model), bf16), jax.ShapeDtypeStruct(wr_t.shape, f32)) + (jax.ShapeDtypeStruct((acts.shape[2], d_model), f32),) * 3,
        in_specs=[hbm, hbm, hbm, hbm, vmem, vmem, vmem, vmem, vmem],
        out_specs=(vmem, vmem, vmem, hbm, hbm, hbm),
        scratch_shapes=[
            pltpu.VMEM((2, 4, 4, tok, d_model), bf16),
            pltpu.VMEM((2, 4, 4, tok, d_model), bf16),
            pltpu.VMEM((2, 4, tok, d_model), bf16),
            pltpu.VMEM((2, 2, 4, tok, d_model), bf16),
            pltpu.VMEM((2, 2, tok, d_model), f32),
            pltpu.VMEM((2, 3, tok, d_model), bf16),
            pltpu.VMEM((2, 2, half, d_model), bf16),
            pltpu.VMEM((2, 2, 2, half, d_model), bf16),
            pltpu.VMEM((2, count * tok, d_model), bf16),
            pltpu.VMEM(acts.shape, bf16),
            pltpu.VMEM((2, 256, d_model), f32),
            pltpu.VMEM((count, 8, 128), f32),
            pltpu.VMEM((count, wr_t.shape[0], 128), bf16),
            pltpu.VMEM((wr_t.shape[0], 128), bf16),
            dma((3, 4)), dma((3,)), dma((2,)), dma((48,)), dma((48,)), dma((count,)), dma((count,)), dma((count,)), dma((count,)),
        ],
        compiler_params=pltpu.CompilerParams(collective_id=1, has_side_effects=True, vmem_limit_bytes=62 * 1024 * 1024),
        name="reduce_back",
    )(y_part.reshape(shape5), du_part.reshape(shape5), all_rows, acts, dg_tiles, u_loc, dy_loc, wr_t, prob_t)


SITES = tuple((tuple(map(int, two[:PAIR.stop])), tuple(map(int, two[PAIR.stop:]))) for two in "0003-1030-0102-3313-3111-2023-3212-2122".split("-"))
UP_SET = (0, 1)


def pick(idx, table):
    out = jnp.int32(table[0])
    for pos in range(1, len(table)):
        out = jnp.where(idx == pos, jnp.int32(table[pos]), out)
    return out


def gather_kernel(etp_size, ring, width, u_ref, dy_ref, ids_ref, wr_ref, w1_hbm, w3_hbm, w2_hbm,
                  y_hbm, du_hbm, all_hbm, act_hbm, dg_out, prob_out,
                  rows, w1, w3, w2, w1_t, w3_t, w2_t, y_buf, du_buf, act_buf, gate_out, gate_in,
                  w_sem, out_sem, keep_sem, send_sem, near_sem, half_sem, peer_sem, gate_send, gate_recv):
    ep, etp = lax.axis_index("ep"), lax.axis_index("etp")
    col, core = ep // 2, ep % 2
    lin = ep * etp_size + etp
    count = ring * 2 * etp_size
    tok, d_model = u_ref.shape
    half = tok // 2
    experts = wr_ref.shape[0]
    local_exp = experts // (2 * ring)
    bf16, f32 = jnp.bfloat16, jnp.float32

    w_copies = [pltpu.make_async_copy(src, dst, w_sem.at[pos]) for pos, (src, dst) in enumerate(((w1_hbm, w1), (w3_hbm, w3), (w2_hbm, w2)))]
    for copy in w_copies:
        copy.start()

    barrier = pltpu.get_barrier_semaphore()

    def other(step):
        dest = lax.rem(lin + step, count)
        return {"ep": dest // etp_size, "etp": lax.rem(dest, etp_size)}, dest

    def greet(step, carry):
        pl.semaphore_signal(barrier, inc=1, device_id=other(step)[0], device_id_type=MESH)
        return carry

    each_other(count, greet)
    logit = lax.dot_general(wr_ref[...], u_ref[...], (((1,), (1,)), ((), ())), preferred_element_type=f32)
    top = jnp.max(logit, axis=0, keepdims=True)
    expo = jnp.exp(logit - top)
    prob = expo / jnp.sum(expo, axis=0, keepdims=True)
    prob_out[...] = jnp.zeros_like(prob_out)
    prob_out[:, :tok] = prob
    ids = ids_ref[...]
    expert_at = lax.broadcasted_iota(jnp.int32, (experts, tok), 0)
    hot = expert_at == ids[0:1]
    for choice in range(1, ids.shape[0]):
        hot = hot | (expert_at == ids[choice:choice + 1])
    gate = jnp.where(hot, prob, 0.0)
    gate_out[...] = jnp.zeros_like(gate_out)
    for group in range(2 * ring):
        gate_out[group, :local_exp, :tok] = gate[group * local_exp:(group + 1) * local_exp]

    pl.semaphore_wait(barrier, count - 1)

    def at_x(step):
        return {"ep": lax.rem(col + step, ring) * 2 + core, "etp": etp}

    def at_y(step):
        return {"ep": ep, "etp": lax.rem(etp + step, etp_size)}

    along_first = (at_y, at_x)
    along_second = (at_x, at_y)
    partner = {"ep": col * 2 + 1 - core, "etp": etp}

    def spot(arr, first, second):
        rel_x, rel_y = (second, first) if arr == 0 else (first, second)
        return lax.rem(col + rel_x, ring), lax.rem(etp + rel_y, etp_size)

    def block(arr, first, second):
        x_at, y_at = spot(arr, first, second)
        return rows.at[arr, x_at, y_at, core]

    sends = []

    def send(src, dst, recv_sem, device):
        slot = len(sends)
        copy = pltpu.make_async_remote_copy(src, dst, send_sem.at[slot], recv_sem, device_id=device, device_id_type=MESH)
        copy.start()
        sends.append(src.shape[0])

    def landed(ref, sem):
        pltpu.make_async_copy(ref, ref, sem).wait()

    def to_second(arr, first, src):
        dst = block(arr, first, 0)
        send(src, dst, near_sem.at[arr, first, 3], along_second[arr](1))
        send(src, dst, near_sem.at[arr, first, 1], along_second[arr](3))

    def to_peer(arr, first, second, src):
        send(src, block(arr, first, second), peer_sem.at[arr, first, second], partner)

    def first_own(arr):
        src = (u_ref, dy_ref)[arr]
        dst = block(arr, 0, 0)
        send(src, dst, near_sem.at[arr, 3, 0], along_first[arr](1))
        send(src, dst, near_sem.at[arr, 1, 0], along_first[arr](3))
        to_peer(arr, 0, 0, src)

    def second_own(arr):
        to_second(arr, 0, (u_ref, dy_ref)[arr])

    def event_first(arr, first):
        ref = block(arr, first, 0)
        landed(ref, near_sem.at[arr, first, 0])
        part = 0 if first == 3 else 1
        piece = ref.at[pl.ds(part * half, half)]
        send(piece, piece, half_sem.at[arr, part], along_first[arr](1 if first == 3 else 3))
        to_peer(arr, first, 0, ref)
        to_second(arr, first, ref)

    def event_far(arr):
        ref = block(arr, 2, 0)
        for part in PAIR:
            landed(ref.at[pl.ds(part * half, half)], half_sem.at[arr, part])
        to_peer(arr, 2, 0, ref)
        to_second(arr, 2, ref)

    def event_near(arr, first):
        for second in (3, 1):
            ref = block(arr, first, second)
            landed(ref, near_sem.at[arr, first, second])
            if (second == 3) == (first in UP_SET):
                send(ref, ref, near_sem.at[arr, first, 2], along_second[arr](1 if second == 3 else 3))
            to_peer(arr, first, second, ref)

    def event_end(arr, first):
        ref = block(arr, first, 2)
        landed(ref, near_sem.at[arr, first, 2])
        to_peer(arr, first, 2, ref)

    def gate_copy(step):
        device, dest = other(step)
        return pltpu.make_async_remote_copy(gate_out.at[dest // etp_size], gate_in.at[lin], gate_send.at[step], gate_recv.at[lin], device_id=device, device_id_type=MESH)

    def start_gate(step, carry):
        gate_copy(step).start()
        return carry

    each_other(count, start_gate)
    gate_in[lin] = gate_out[ep]

    first_own(0)
    first_own(1)
    second_own(1)
    second_own(0)
    for arr, ref in enumerate((u_ref, dy_ref)):
        rows[arr, col, etp, core] = ref[...]

    lane_tile = 128
    for copy in w_copies:
        copy.wait()

    def flip(pos, carry):
        span = pl.ds(pl.multiple_of(pos * lane_tile, lane_tile), lane_tile)
        for src, dst in ((w1, w1_t), (w3, w3_t), (w2, w2_t)):
            dst[span, :] = src[:, span].T
        return carry

    lax.fori_loop(0, d_model // lane_tile, flip, 0)

    def wait_gate(step, carry):
        src = lax.rem(lin + step, count)
        landed(gate_in.at[src], gate_recv.at[src])
        return carry

    for first in (3, 1):
        for arr in PAIR:
            event_first(arr, first)

    def peer_wait(arr, site):
        first, second = (site[1], site[0]) if arr == 0 else (site[0], site[1])
        x_at, y_at = spot(arr, first, second)
        landed(rows.at[arr, x_at, y_at, 1 - core], peer_sem.at[arr, first, second])

    def event_gate():
        each_other(count, wait_gate)

    def both(event, *args):
        return [(event, (arr,) + args) for arr in PAIR]

    plan = {
        (0, 1): [(event_gate, ())] + both(event_near, 0),
        (0, 2): both(event_far),
        (1, 1): both(event_near, 3),
        (2, 0): both(event_end, 0),
        (2, 2): both(event_near, 1),
        (3, 2): both(event_near, 2),
        (4, 1): both(event_end, 3),
        (5, 1): both(event_end, 1) + both(event_end, 2),
    }

    def run_events(unit, point):
        for pos in range(len(SITES)):
            todo = list(plan.get((pos, point), []))
            if point < 2:
                todo += [(peer_wait, (point, site)) for site in SITES[pos]]
            if todo:
                @pl.when(unit == pos)
                def _():
                    for event, args in todo:
                        event(*args)

    def out_copies(slot, sites):
        copies = []
        for pos, (x_at, y_at) in enumerate(sites):
            base = pos * 2
            copies.append(pltpu.make_async_copy(y_buf.at[slot, pl.ds(base, 2)], y_hbm.at[x_at, :, y_at], out_sem.at[slot, pos, 0]))
            copies.append(pltpu.make_async_copy(du_buf.at[slot, pl.ds(base, 2)], du_hbm.at[x_at, :, y_at], out_sem.at[slot, pos, 1]))
            for kind in range(3):
                copies.append(pltpu.make_async_copy(act_buf.at[slot, kind, pl.ds(base, 2)], act_hbm.at[kind, x_at, y_at], out_sem.at[slot, pos, 2 + kind]))
        return copies

    def sites_of(unit):
        out = []
        for pos in PAIR:
            rel_x = pick(unit, [entry[pos][0] for entry in SITES])
            rel_y = pick(unit, [entry[pos][1] for entry in SITES])
            out.append((lax.rem(col + rel_x, ring), lax.rem(etp + rel_y, etp_size)))
        return out

    def load(arr, sites):
        return jnp.concatenate([rows[arr, x_at, y_at].reshape(2 * tok, d_model) for x_at, y_at in sites], axis=0)

    def mm(lhs, rhs):
        return jnp.dot(lhs, rhs, preferred_element_type=f32)

    def unit_step(unit, carry):
        slot = lax.rem(unit, 2)
        sites = sites_of(unit)
        run_events(unit, 0)

        @pl.when(unit >= 2)
        def _():
            for copy in out_copies(slot, sites):
                copy.wait()

        x_rows = load(0, sites)
        h1 = mm(x_rows, w1_t[...]).astype(bf16).astype(f32)
        h3 = mm(x_rows, w3_t[...]).astype(bf16).astype(f32)
        run_events(unit, 1)
        for arr in PAIR:
            for pos, (x_at, y_at) in enumerate(sites):
                pltpu.make_async_copy(rows.at[arr, x_at, y_at], all_hbm.at[arr, x_at, y_at], keep_sem.at[slot, arr, pos]).start()
        q = mm(load(1, sites), w2_t[...])
        cols = []
        lins = []
        for x_at, y_at in sites:
            for side in PAIR:
                src = (x_at * 2 + side) * etp_size + y_at
                lins.append(src)
                cols.append(gate_in[src].T[:tok])
        gate_cols = jnp.concatenate(cols, axis=0)
        lane = lax.broadcasted_iota(jnp.int32, q.shape, 1)
        wide = jnp.broadcast_to(gate_cols[:, local_exp - 1:local_exp], q.shape)
        for pos in range(local_exp - 2, -1, -1):
            wide = jnp.where(lane < (pos + 1) * width, gate_cols[:, pos:pos + 1], wide)
        live = wide > 0
        sig = jax.nn.sigmoid(h1)
        silu = h1 * sig
        act = jnp.where(live, (silu * h3).astype(bf16).astype(f32), 0.0)
        ga = (wide * act).astype(bf16)
        da = (wide * q).astype(bf16).astype(f32)
        dh1 = jnp.where(live, da * h3 * sig * (1.0 + h1 * (1.0 - sig)), 0.0).astype(bf16)
        dh3 = jnp.where(live, da * silu, 0.0).astype(bf16)
        prod = act * q
        dg_wide = jnp.zeros((prod.shape[0], lane_tile), f32)
        lane_s = lax.broadcasted_iota(jnp.int32, dg_wide.shape, 1)
        for pos in range(local_exp):
            total = jnp.zeros_like(dg_wide)
            for tile in range(pos * width // lane_tile, -(-(pos + 1) * width // lane_tile)):
                piece = prod[:, tile * lane_tile:(tile + 1) * lane_tile]
                low, high = pos * width - tile * lane_tile, (pos + 1) * width - tile * lane_tile
                if low > 0:
                    piece = jnp.where(lane_s >= low, piece, 0.0)
                if high < lane_tile:
                    piece = jnp.where(lane_s < high, piece, 0.0)
                total = total + piece
            dg_wide = jnp.where(lane_s == pos, jnp.sum(total, axis=1, keepdims=True), dg_wide)
        for pos, src in enumerate(lins):
            dg_out[src] = jnp.concatenate([dg_wide[pos * tok:(pos + 1) * tok].T[:8], jnp.zeros((8, lane_tile - tok), f32)], axis=1)
        for kind, val in enumerate((dh1, dh3, ga)):
            act_buf[slot, kind] = val.reshape(4, tok, val.shape[1])
        run_events(unit, 2)
        y_buf[slot] = mm(act_buf[slot, 2].reshape(4 * tok, -1), w2[...]).astype(bf16).reshape(4, tok, d_model)
        dx = mm(act_buf[slot, 0].reshape(4 * tok, -1), w1[...]) + mm(act_buf[slot, 1].reshape(4 * tok, -1), w3[...])
        du_buf[slot] = dx.astype(bf16).reshape(4, tok, d_model)
        for copy in out_copies(slot, sites):
            copy.start()
        for arr in PAIR:
            for pos, (x_at, y_at) in enumerate(sites):
                pltpu.make_async_copy(rows.at[arr, x_at, y_at], all_hbm.at[arr, x_at, y_at], keep_sem.at[slot, arr, pos]).wait()
        return carry

    units = len(SITES)
    lax.fori_loop(0, units, unit_step, 0)
    for unit in (units - 2, units - 1):
        for copy in out_copies(unit % 2, sites_of(unit)):
            copy.wait()
    for slot, size in enumerate(sends):
        ref = rows.at[0, 0, 0, 0, pl.ds(0, size)]
        landed(ref, send_sem.at[slot])

    def drain(step, carry):
        gate_copy(step).wait_send()
        return carry

    each_other(count, drain)


def gather_call(mesh, u_loc, dy_loc, ids_t, wr_t, w1, w3, w2):
    etp_size, ep_size = mesh.shape["etp"], mesh.shape["ep"]
    tok, d_model = u_loc.shape
    experts, inner = wr_t.shape[0], w1.shape[0]
    count, ring = etp_size * ep_size, ep_size // 2
    assert ring == 4 and etp_size == 4
    width = inner // (experts // ep_size)
    vmem = pl.BlockSpec(memory_space=pltpu.VMEM)
    hbm = pl.BlockSpec(memory_space=pl.ANY)
    bf16, f32 = jnp.bfloat16, jnp.float32
    dma = pltpu.SemaphoreType.DMA
    part = jax.ShapeDtypeStruct((ring, 2, etp_size, tok, d_model), bf16)
    return pl.pallas_call(
        functools.partial(gather_kernel, etp_size, ring, width),
        out_shape=(part, part, jax.ShapeDtypeStruct((2, ring, etp_size, 2, tok, d_model), bf16), jax.ShapeDtypeStruct((3, ring, etp_size, 2, tok, inner), bf16),
                   jax.ShapeDtypeStruct((count, 8, 128), f32), jax.ShapeDtypeStruct((experts, 128), f32)),
        in_specs=[vmem, vmem, vmem, vmem, hbm, hbm, hbm],
        out_specs=(hbm, hbm, hbm, hbm, vmem, vmem),
        scratch_shapes=[
            pltpu.VMEM((2, ring, etp_size, 2, tok, d_model), bf16),
            pltpu.VMEM((inner, d_model), bf16), pltpu.VMEM((inner, d_model), bf16), pltpu.VMEM((inner, d_model), bf16),
            pltpu.VMEM((d_model, inner), bf16), pltpu.VMEM((d_model, inner), bf16), pltpu.VMEM((d_model, inner), bf16),
            pltpu.VMEM((2, 4, tok, d_model), bf16), pltpu.VMEM((2, 4, tok, d_model), bf16), pltpu.VMEM((2, 3, 4, tok, inner), bf16),
            pltpu.VMEM((ep_size, 8, 128), f32), pltpu.VMEM((count, 8, 128), f32),
            dma((3,)), dma((2, 2, 5)), dma((2, 2, 2)), dma((72,)), dma((2, 4, 4)), dma((2, 2)), dma((2, 4, 4)), dma((count,)), dma((count,)),
        ],
        compiler_params=pltpu.CompilerParams(collective_id=0, has_side_effects=True, vmem_limit_bytes=60 * 1024 * 1024),
        name="gather_experts",
    )(u_loc, dy_loc, ids_t, wr_t, w1, w3, w2)


def solution(mesh):
    tok_spec = P(("dp", "ep", "etp"), None)
    col_spec = P("ep", None, "etp")
    row_spec = P("ep", "etp", None)
    in_specs = (tok_spec, tok_spec, tok_spec, P(None, None), col_spec, col_spec, row_spec)
    out_specs = (tok_spec, tok_spec, P(("dp", "ep"), None, "etp"), P(("dp", "ep"), None, "etp"), P(("dp", "ep"), "etp", None), P("dp", None))

    def device_step(u_loc, dy_loc, ids_loc, w_router, w_gate, w_up, w_down):
        local_exp, d_model, width = w_gate.shape
        inner = local_exp * width
        w1 = jnp.swapaxes(w_gate, 1, 2).reshape(inner, d_model)
        w3 = jnp.swapaxes(w_up, 1, 2).reshape(inner, d_model)
        w2 = w_down.reshape(inner, d_model)
        y_part, du_part, both_all, acts, dg_tiles, prob_t = gather_call(mesh, u_loc, dy_loc, ids_loc.T, w_router.T, w1, w3, w2)
        both_all = both_all.reshape(2, -1, d_model)
        acts = acts.reshape(3, -1, inner)
        y_loc, du_loc, dwr_t, dw1, dw3, dw2 = reduce_call(mesh, y_part, du_part, both_all, acts, dg_tiles, u_loc, dy_loc, w_router.T, prob_t)
        unfold = lambda d: jnp.swapaxes(d.reshape(local_exp, width, d_model), 1, 2)
        return y_loc, du_loc, unfold(dw1), unfold(dw3), dw2.reshape(local_exp, width, d_model), dwr_t.T

    return jax.shard_map(device_step, mesh=mesh, in_specs=in_specs, out_specs=out_specs, check_vma=False)
```

time: 225 us -> 139 us (0.62)
  matrix products: 80.1 us -> 0 us
  Pallas kernels: 46.1 us -> 123 us
  waiting for transfers between devices: 44.6 us -> 0 us
  blocking collectives: 33.3 us -> 0 us
  between operations: 14.3 us -> 0.66 us
  local copies, waits for them, and re-layouts: 2.8 us -> 14.6 us
  other arithmetic: 3.95 us -> 0.01 us
    dot_general x10 -> x0, matrix products: 80.1 us -> none  [the longest x9 79 us: dot_f32(): lax.dot_general(lhs, rhs, (contract, ((), ())), preferred_element_type=jn...]
    pallas_call x0 -> x1, Pallas kernels: none -> 75.5 us  [gather_call(): pl.pallas_call(functools.partial(gather_kernel, etp_size, ring, width), o...]
    all_gather x2 -> x0, waiting for transfers between devices: 43.1 us -> none  [the longest x1 29.1 us: device_step(): dy_all = lax.all_gather(dy_loc, axes, axis=0, tiled=True)]
    all_gather x1 -> x0, blocking collectives: 33.3 us -> none  [device_step(): gate_all = lax.all_gather(gate_loc, axes, axis=0, tiled=True)]
    unnamed x38 -> x14, local copies, waits for them, and re-layouts: 2.31 us -> 14.6 us
    reduce_sum x2 -> x0, other arithmetic: 3.23 us -> none  [the longest x1 3.2 us: device_step(): dgate = jnp.sum((act * q).reshape(-1, local_exp, width), axis=2)]
  transfers between devices with their start and end apart: 2 -> 0, of which waited for: 2 -> 0; matrix products, arithmetic and copies ran while one was open for 8% -> 0% of each run, Pallas kernels for 0% -> 0%
where the time goes in v3:
time: 139 us
  Pallas kernels  123 us (88%)
  local copies, waits for them, and re-layouts  14.6 us (11%)
    pallas_call x1, Pallas kernels, gather_call(): pl.pallas_call(functools.partial(gather_kernel, etp_size, ring, width), o...  75.5 us
    pallas_call x1, Pallas kernels, reduce_call(): pl.pallas_call(functools.partial(reduce_kernel, etp_size), out_shape=(jax...  48 us
    unnamed x14, local copies, waits for them, and re-layouts  14.6 us

profile of v3, /device:TPU:97, one launch (start us, length us, event | category | flops | bytes accessed | tf_op | source)
XLA Modules:
  0.0 138.8 jit_solution(12986028293100083050)
XLA Ops:
  0.6 75.5 %gather_experts.1 = (bf16[4,2,4,64,1536]{4,3,2,1,0:T(8,128)(2,1)}, bf16[4,2,4,64,1536]{4,3,2,1,0:T(8,128)(2,1)}, bf16[2,4,4,2,64,1536]{5,4,3,2,1,0:T(8,128)(2,1)...) custom-call(bf16[64,1536]{1,0:T(8,128)(2,1)} %u_ref.3, ...), custom_call_target="tpu_custom_call" | custom-call | tf_op jit(solution)/shard_map/gather_experts/pallas_call | solution.py:640
  76.1 48.0 %reduce_back.1 = (bf16[64,1536]{1,0:T(8,128)(2,1)}, bf16[64,1536]{1,0:T(8,128)(2,1)}, f32[32,1536]{1,0:T(8,128)}, f32[768,1536]{1,0:T(8,128)}, f32[768,1536]{1,0:T(8,128)}, /*index=5*/f32[768,1536]{1,0:T(8,128)}) custom-call(bf16[4,2,4,64,1536]{4,3,2,1,0:T(8,128)(2,1)} %get-tuple-element.18.y_hbm, bf16[4,2,4,64,1536]{4,3,2,1,0:T(8,128)(2,1)} %get-tuple-element.19.du_hbm, ...), custom_call_target="tpu_custom_call" | custom-call | tf_op jit(solution)/shard_map/reduce_back/pallas_call | solution.py:288
  124.1 1.6 %copy.19 = bf16[64,1536]{1,0:T(8,128)(2,1)} copy(bf16[64,1536]{1,0:T(8,128)(2,1)} %get-tuple-element.36) | data formatting | bytes 393216
  125.7 1.6 %copy.20 = bf16[64,1536]{1,0:T(8,128)(2,1)} copy(bf16[64,1536]{1,0:T(8,128)(2,1)} %get-tuple-element.37) | data formatting | bytes 393216
  127.4 0.0 copy-start
  127.4 0.0 slice-start
  127.4 5.2 %copy.21 = f32[4,1536,192]{1,2,0:T(8,128)} copy(f32[4,1536,192]{1,2,0:T(8,128)} %bitcast.25) | data formatting | bytes 9437184
  132.6 0.0 copy-done
  132.6 0.0 slice-start.1
  132.6 2.4 %copy.22 = f32[4,1536,192]{1,2,0:T(8,128)} copy(f32[4,1536,192]{1,2,0:T(8,128)S(1)} %bitcast.24) | data formatting | bytes 9437184
  135.0 0.4 slice-done
  135.3 0.6 slice-done.1
  135.9 0.0 copy-start.1
  135.9 2.2 %copy.23 = f32[4,192,1536]{2,1,0:T(8,128)} copy(f32[4,192,1536]{2,1,0:T(8,128)S(1)} %bitcast.23) | data formatting | bytes 9437184
  138.1 0.0 copy-done.1
  138.1 0.7 copy.24
  (1 shorter events, 0.0 us)
Async XLA Ops:
  127.4 5.2 %copy-start = (f32[768,1536]{1,0:T(8,128)S(1)}, f32[768,1536]{1,0:T(8,128)}, u32[]{:S(2)}) copy-start(f32[768,1536]{1,0:T(8,128)} %get-tuple-element.27) | copy-start | bytes 14155780
  127.4 8.0 %slice-start = ((s8[4718592]{0:T(1024)(128)(4,1)}), s8[4194304]{0:T(1024)(128)(4,1)S(1)}, s32[]{:S(2)}) async-start(s8[4718592]{0:T(1024)(128)(4,1)} %bitcast.21), calls=%async_computation | async-start | bytes 8388608
  132.6 3.3 %slice-start.1 = ((s8[4718592]{0:T(1024)(128)(4,1)}), s8[524288]{0:T(1024)(128)(4,1)S(1)}, s32[]{:S(2)}) async-start(s8[4718592]{0:T(1024)(128)(4,1)} %bitcast.21), calls=%async_computation.1 | async-start | bytes 1048576
  135.9 2.2 %copy-start.1 = (f32[32,1536]{1,0:T(8,128)S(1)}, f32[32,1536]{1,0:T(8,128)}, u32[]{:S(2)}) copy-start(f32[32,1536]{1,0:T(8,128)} %get-tuple-element.29) | copy-start | bytes 589828

commit v4 on v1

v4 whole, which is shorter than its diff:
```python
import functools

import jax
import jax.numpy as jnp
from jax import lax
from jax.experimental import pallas as pl
from jax.experimental.pallas import tpu as pltpu
from jax.sharding import PartitionSpec as P

MESH = pl.DeviceIdType.MESH
PAIR = range(2)


def each_other(count, step):
    lax.fori_loop(1, count, step, 0)


SITES = tuple((tuple(map(int, two[:PAIR.stop])), tuple(map(int, two[PAIR.stop:]))) for two in "0003-0110-3033-1331-1102-2023-2112-3222".split("-"))
UP_SET = (0, 1)


def pick(idx, table):
    out = jnp.int32(table[0])
    for pos in range(1, len(table)):
        out = jnp.where(idx == pos, jnp.int32(table[pos]), out)
    return out


def block_kernel(etp_size, ring, width, u_ref, dy_ref, ids_ref, wr_ref, w1_hbm, w3_hbm, w2_hbm,
                 y_out, du_out, dwr_out, dw1_hbm, dw3_hbm, dw2_hbm, act_hbm,
                 rows, w1, w3, w2, wide, y_buf, du_buf, act_buf, h_buf, gate_out, gate_in, dg_out, prob_ref,
                 mine, peer, relay, inbox, total, stage, relay2, inbox2, dw_buf, dg_in, dl_in, dl_out,
                 w_sem, act_sem, send_sem, near_sem, half_sem, peer_sem, gate_send, gate_recv,
                 swap_send, swap_sem, back_send, back_recv, load_sem, dw_sem, dg_send, dg_recv, dl_send, dl_recv):
    ep, etp = lax.axis_index("ep"), lax.axis_index("etp")
    col, core = ep // 2, ep % 2
    lin = ep * etp_size + etp
    count = ring * 2 * etp_size
    tok, d_model = u_ref.shape
    half = tok // 2
    experts = wr_ref.shape[0]
    local_exp = experts // (2 * ring)
    bf16, f32 = jnp.bfloat16, jnp.float32

    w_copies = [pltpu.make_async_copy(src, dst, w_sem.at[pos]) for pos, (src, dst) in enumerate(((w1_hbm, w1), (w3_hbm, w3), (w2_hbm, w2)))]
    for copy in w_copies:
        copy.start()

    barrier = pltpu.get_barrier_semaphore()

    def other(step):
        dest = lax.rem(lin + step, count)
        return {"ep": dest // etp_size, "etp": lax.rem(dest, etp_size)}, dest

    def greet(step, carry):
        pl.semaphore_signal(barrier, inc=1, device_id=other(step)[0], device_id_type=MESH)
        return carry

    each_other(count, greet)
    logit = lax.dot_general(wr_ref[...], u_ref[...], (((1,), (1,)), ((), ())), preferred_element_type=f32)
    top = jnp.max(logit, axis=0, keepdims=True)
    expo = jnp.exp(logit - top)
    prob = expo / jnp.sum(expo, axis=0, keepdims=True)
    prob_ref[...] = jnp.zeros_like(prob_ref)
    prob_ref[:, :tok] = prob
    ids = ids_ref[...]
    expert_at = lax.broadcasted_iota(jnp.int32, (experts, tok), 0)
    hot = expert_at == ids[0:1]
    for choice in range(1, ids.shape[0]):
        hot = hot | (expert_at == ids[choice:choice + 1])
    gate = jnp.where(hot, prob, 0.0)
    gate_out[...] = jnp.zeros_like(gate_out)
    for group in range(2 * ring):
        gate_out[group, :local_exp, :tok] = gate[group * local_exp:(group + 1) * local_exp]

    pl.semaphore_wait(barrier, count - 1)

    def at_x(step):
        return {"ep": lax.rem(col + step, ring) * 2 + core, "etp": etp}

    def at_y(step):
        return {"ep": ep, "etp": lax.rem(etp + step, etp_size)}

    along_first = (at_y, at_x)
    along_second = (at_x, at_y)
    partner = {"ep": col * 2 + 1 - core, "etp": etp}

    def spot(arr, first, second):
        rel_x, rel_y = (second, first) if arr == 0 else (first, second)
        return lax.rem(col + rel_x, ring), lax.rem(etp + rel_y, etp_size)

    def block(arr, first, second):
        x_at, y_at = spot(arr, first, second)
        return rows.at[arr, x_at, y_at, core]

    sends = []

    def send(src, dst, recv_sem, device):
        slot = len(sends)
        copy = pltpu.make_async_remote_copy(src, dst, send_sem.at[slot], recv_sem, device_id=device, device_id_type=MESH)
        copy.start()
        sends.append(src.shape[0])

    def landed(ref, sem):
        pltpu.make_async_copy(ref, ref, sem).wait()

    def to_second(arr, first, src):
        dst = block(arr, first, 0)
        send(src, dst, near_sem.at[arr, first, 3], along_second[arr](1))
        send(src, dst, near_sem.at[arr, first, 1], along_second[arr](3))

    def to_peer(arr, first, second, src):
        send(src, block(arr, first, second), peer_sem.at[arr, first, second], partner)

    def first_own(arr):
        src = (u_ref, dy_ref)[arr]
        dst = block(arr, 0, 0)
        send(src, dst, near_sem.at[arr, 3, 0], along_first[arr](1))
        send(src, dst, near_sem.at[arr, 1, 0], along_first[arr](3))
        to_peer(arr, 0, 0, src)

    def second_own(arr):
        to_second(arr, 0, (u_ref, dy_ref)[arr])

    def event_first(arr, first):
        ref = block(arr, first, 0)
        landed(ref, near_sem.at[arr, first, 0])
        part = 0 if first == 3 else 1
        piece = ref.at[pl.ds(part * half, half)]
        send(piece, piece, half_sem.at[arr, part], along_first[arr](1 if first == 3 else 3))
        to_peer(arr, first, 0, ref)
        to_second(arr, first, ref)

    def event_far(arr):
        ref = block(arr, 2, 0)
        for part in PAIR:
            landed(ref.at[pl.ds(part * half, half)], half_sem.at[arr, part])
        to_peer(arr, 2, 0, ref)
        to_second(arr, 2, ref)

    def event_relay(arr, first):
        second = 3 if first in UP_SET else 1
        ref = block(arr, first, second)
        send(ref, ref, near_sem.at[arr, first, 2], along_second[arr](4 - second))

    def event_near(arr, first):
        for second in (3, 1):
            ref = block(arr, first, second)
            landed(ref, near_sem.at[arr, first, second])
            to_peer(arr, first, second, ref)

    def event_end(arr, first):
        ref = block(arr, first, 2)
        landed(ref, near_sem.at[arr, first, 2])
        to_peer(arr, first, 2, ref)

    def gate_copy(step):
        device, dest = other(step)
        return pltpu.make_async_remote_copy(gate_out.at[dest // etp_size], gate_in.at[lin], gate_send.at[step], gate_recv.at[lin], device_id=device, device_id_type=MESH)

    def start_gate(step, carry):
        gate_copy(step).start()
        return carry

    each_other(count, start_gate)
    gate_in[lin] = gate_out[ep]

    first_own(0)
    first_own(1)
    second_own(1)
    second_own(0)
    for arr, ref in enumerate((u_ref, dy_ref)):
        rows[arr, col, etp, core] = ref[...]

    lane_tile = 128
    for copy in w_copies:
        copy.wait()

    def flip(pos, carry):
        span = pl.ds(pl.multiple_of(pos * lane_tile, lane_tile), lane_tile)
        for src, dst in ((w1, wide.at[0]), (w3, wide.at[1]), (w2, wide.at[2])):
            dst[span, :] = src[:, span].T
        return carry

    lax.fori_loop(0, d_model // lane_tile, flip, 0)

    def wait_gate(step, carry):
        src = lax.rem(lin + step, count)
        landed(gate_in.at[src], gate_recv.at[src])
        return carry

    for first in (3, 1):
        for arr in PAIR:
            event_first(arr, first)

    def peer_wait(arr, site):
        first, second = (site[1], site[0]) if arr == 0 else (site[0], site[1])
        x_at, y_at = spot(arr, first, second)
        landed(rows.at[arr, x_at, y_at, 1 - core], peer_sem.at[arr, first, second])

    def event_gate():
        each_other(count, wait_gate)

    def both(event, *args):
        return [(event, (arr,) + args) for arr in PAIR]

    spots = ((col, etp), (etp, col))
    back_sends = []
    back_slot = {}

    def back(key, src, dst, device):
        slot = back_slot.setdefault(key, len(back_slot))
        copy = pltpu.make_async_remote_copy(src, dst, back_send.at[slot], back_recv.at[slot], device_id=device, device_id_type=MESH)
        copy.start()
        back_sends.append((slot, src.shape[0]))

    def arrive(key, ref):
        landed(ref, back_recv.at[back_slot[key]])

    def cell(ref, arr, first, sub):
        return ref.at[arr, lax.rem(spots[arr][0] + first, ring), lax.rem(spots[arr][1] + sub, ring)]

    def value(arr, first, sub):
        landed(cell(peer, arr, first, sub), swap_sem.at[arr, first, sub])
        return cell(mine, arr, first, sub)[...].astype(f32) + cell(peer, arr, first, sub)[...].astype(f32)

    def put(arr, first, sub, val):
        ref = cell(mine, arr, first, sub)
        ref[...] = val.astype(bf16)
        return ref

    far_slot = {2: 0, 1: 1, 3: 2, 0: 3}

    def back_far(arr, sub):
        device = along_stage(arr, sub in (2, 1))
        back(("far", arr, sub), put(arr, 2, sub, value(arr, 2, sub)), relay.at[arr, far_slot[sub]], device)

    def along_stage(arr, right):
        return along_second[arr](1 if right else 3)

    def back_direct(arr, sub):
        right = sub in (3, 0)
        first = 1 if right else 3
        back(("left" if right else "right", arr, sub), put(arr, first, sub, value(arr, first, sub)), inbox.at[arr, 0 if right else 1, sub], along_stage(arr, right))

    def back_relay(arr, sub):
        right = sub in (2, 1)
        first = 1 if right else 3
        incoming = relay.at[arr, far_slot[sub]]
        arrive(("far", arr, sub), incoming)
        val = value(arr, first, sub) + incoming[...].astype(f32)
        back(("left" if right else "right", arr, sub), put(arr, first, sub, val), inbox.at[arr, 0 if right else 1, sub], along_stage(arr, right))

    plan = {
        (0, 1): [(event_gate, ())] + both(event_near, 0),
        (0, 2): both(event_far) + both(event_relay, 0),
        (1, 2): both(event_near, 3) + both(event_relay, 3),
        (2, 1): both(event_near, 1) + both(event_relay, 1),
        (3, 1): both(event_near, 2) + both(event_relay, 2),
        (4, 0): both(back_direct, 0),
        (4, 1): both(event_end, 0),
        (4, 2): both(event_end, 3) + both(back_direct, 3),
        (4, 3): both(back_direct, 1),
        (5, 1): both(event_end, 1) + both(event_end, 2),
        (5, 2): [(back_far, (1, 0))],
        (6, 1): both(back_far, 0)[:1] + [(back_far, (0, 3)), (back_direct, (1, 2))],
        (7, 1): both(back_far, 1),
    }

    def run_events(unit, point):
        for pos in range(len(SITES)):
            todo = list(plan.get((pos, point), []))
            if point < 2:
                todo += [(peer_wait, (point, site)) for site in SITES[pos]]
            if todo:
                @pl.when(unit == pos)
                def _():
                    for event, args in todo:
                        event(*args)

    def act_copies(sites):
        copies = []
        for pos, (x_at, y_at) in enumerate(sites):
            site = (x_at * etp_size + y_at) * 2 * tok
            for kind in range(3):
                copies.append(pltpu.make_async_copy(act_buf.at[kind, pl.ds(pos * 2 * tok, 2 * tok)], act_hbm.at[kind, pl.ds(pl.multiple_of(site, 2 * tok), 2 * tok)], act_sem.at[pos, kind]))
        return copies

    def swap_copies(slot, sites, rels):
        copies = []
        for pos, (x_at, y_at) in enumerate(sites):
            rel_x, rel_y = rels[pos]
            away = 2 * pos + 1 - core
            copies.append(pltpu.make_async_remote_copy(y_buf.at[slot, away], peer.at[0, x_at, y_at], swap_send.at[slot, pos, 0], swap_sem.at[0, rel_x, rel_y], device_id=partner, device_id_type=MESH))
            copies.append(pltpu.make_async_remote_copy(du_buf.at[slot, away], peer.at[1, y_at, x_at], swap_send.at[slot, pos, 1], swap_sem.at[1, rel_y, rel_x], device_id=partner, device_id_type=MESH))
        return copies

    def wait_swaps(slot):
        for pos in PAIR:
            landed(y_buf.at[0, 0], swap_send.at[slot, pos, 0])
            landed(du_buf.at[0, 0], swap_send.at[slot, pos, 1])

    def sites_of(unit):
        out = []
        rels = []
        for pos in PAIR:
            rel_x = pick(unit, [entry[pos][0] for entry in SITES])
            rel_y = pick(unit, [entry[pos][1] for entry in SITES])
            out.append((lax.rem(col + rel_x, ring), lax.rem(etp + rel_y, etp_size)))
            rels.append((rel_x, rel_y))
        return out, rels

    def load(arr, sites):
        return jnp.concatenate([rows[arr, x_at, y_at].reshape(2 * tok, d_model) for x_at, y_at in sites], axis=0)

    def mm(lhs, rhs):
        return jnp.dot(lhs, rhs, preferred_element_type=f32)

    def unit_step(unit, carry):
        slot = lax.rem(unit, 2)
        sites, rels = sites_of(unit)
        run_events(unit, 0)

        @pl.when(unit >= 2)
        def _():
            wait_swaps(slot)

        x_rows = load(0, sites)
        h_buf[0] = mm(x_rows, wide[0, :d_model]).astype(bf16)
        h_buf[1] = mm(x_rows, wide[1, :d_model]).astype(bf16)
        run_events(unit, 1)
        @pl.when(unit >= 1)
        def _():
            for copy in act_copies(sites):
                copy.wait()

        q = mm(load(1, sites), wide[2, :d_model])
        cols = []
        lins = []
        for x_at, y_at in sites:
            for side in PAIR:
                src = (x_at * 2 + side) * etp_size + y_at
                lins.append(src)
                cols.append(gate_in[src].T[:tok])
        gate_cols = jnp.concatenate(cols, axis=0)
        lane = lax.broadcasted_iota(jnp.int32, q.shape, 1)
        spread = jnp.broadcast_to(gate_cols[:, local_exp - 1:local_exp], q.shape)
        for pos in range(local_exp - 2, -1, -1):
            spread = jnp.where(lane < (pos + 1) * width, gate_cols[:, pos:pos + 1], spread)
        live = spread > 0
        h1 = jnp.where(live, h_buf[0].astype(f32), 0.0)
        h3 = jnp.where(live, h_buf[1].astype(f32), 0.0)
        sig = jax.nn.sigmoid(h1)
        silu = h1 * sig
        act = (silu * h3).astype(bf16).astype(f32)
        ga = (spread * act).astype(bf16)
        act_buf[2] = ga
        y_buf[slot] = mm(ga, w2[...]).astype(bf16).reshape(4, tok, d_model)
        q = jnp.where(live, q, 0.0)
        da = (spread * q).astype(bf16).astype(f32)
        act_buf[0] = (da * h3 * (sig + silu * (1.0 - sig))).astype(bf16)
        act_buf[1] = (da * silu).astype(bf16)
        prod = act * q
        dg_wide = jnp.zeros((prod.shape[0], lane_tile), f32)
        lane_s = lax.broadcasted_iota(jnp.int32, dg_wide.shape, 1)
        for pos in range(local_exp):
            part_sum = jnp.zeros_like(dg_wide)
            for tile in range(pos * width // lane_tile, -(-(pos + 1) * width // lane_tile)):
                piece = prod[:, tile * lane_tile:(tile + 1) * lane_tile]
                low, high = pos * width - tile * lane_tile, (pos + 1) * width - tile * lane_tile
                if low > 0:
                    piece = jnp.where(lane_s >= low, piece, 0.0)
                if high < lane_tile:
                    piece = jnp.where(lane_s < high, piece, 0.0)
                part_sum = part_sum + piece
            dg_wide = jnp.where(lane_s == pos, jnp.sum(part_sum, axis=1, keepdims=True), dg_wide)
        for pos, src in enumerate(lins):
            dg_out[src] = jnp.concatenate([dg_wide[pos * tok:(pos + 1) * tok].T[:8], jnp.zeros((8, lane_tile - tok), f32)], axis=1)
        run_events(unit, 2)
        run_events(unit, 3)
        dx = mm(act_buf[0], w1[...]) + mm(act_buf[1], w3[...])
        du_buf[slot] = dx.astype(bf16).reshape(4, tok, d_model)
        for copy in act_copies(sites) + swap_copies(slot, sites, rels):
            copy.start()
        for pos, (x_at, y_at) in enumerate(sites):
            mine[0, x_at, y_at] = y_buf[slot, 2 * pos + core]
            mine[1, y_at, x_at] = du_buf[slot, 2 * pos + core]
        return carry

    lax.fori_loop(0, len(SITES), unit_step, 0)

    def dg_copy(step):
        device, dest = other(step)
        return pltpu.make_async_remote_copy(dg_out.at[dest], dg_in.at[lin], dg_send.at[step], dg_recv.at[lin], device_id=device, device_id_type=MESH)

    def dl_copy(step):
        device, dest = other(step)
        return pltpu.make_async_remote_copy(dl_out, dl_in.at[lin], dl_send.at[step], dl_recv.at[lin], device_id=device, device_id_type=MESH)

    def start_dg(step, carry):
        dg_copy(step).start()
        return carry

    each_other(count, start_dg)
    dg_in[lin] = dg_out[lin]
    for copy in act_copies(sites_of(0)[0]):
        copy.wait()
    act_loads = [pltpu.make_async_copy(act_hbm.at[kind], wide.at[kind], load_sem.at[kind]) for kind in range(3)]
    for copy in act_loads:
        copy.start()
    dw_outs = (dw1_hbm, dw3_hbm, dw2_hbm)
    inner = dw1_hbm.shape[0]
    chunk = dw_buf.shape[1]
    chunks = inner // chunk
    pending = {}
    todo = list(range(3 * chunks))

    def dw_steps(number):
        for _ in range(number):
            index = todo.pop(0)
            kind, part = divmod(index, chunks)
            if part == 0:
                act_loads[kind].wait()
            slot = index % 2
            if slot in pending:
                pending[slot].wait()
            lhs = wide[kind, :, part * chunk:(part + 1) * chunk]
            rhs = rows[kind // 2].reshape(count * tok, d_model)
            dw_buf[slot] = lax.dot_general(lhs, rhs, (((0,), (0,)), ((), ())), preferred_element_type=f32)
            pending[slot] = pltpu.make_async_copy(dw_buf.at[slot], dw_outs[kind].at[pl.ds(part * chunk, chunk)], dw_sem.at[slot])
            pending[slot].start()

    back_far(0, 2)
    back_far(1, 2)
    back_far(1, 3)
    back_direct(0, 2)
    dw_steps(2)
    for arr, sub in ((0, 0), (1, 0), (0, 3), (0, 1), (1, 1)):
        back_relay(arr, sub)

    def wait_dg(step, carry):
        src = lax.rem(lin + step, count)
        landed(dg_in.at[src], dg_recv.at[src])
        return carry

    each_other(count, wait_dg)
    tiles = []
    for group in range(2 * ring):
        tile = dg_in[group * etp_size]
        for part in range(1, etp_size):
            tile = tile + dg_in[group * etp_size + part]
        tiles.append(tile[:local_exp])
    d_gate = jnp.concatenate(tiles, axis=0)
    prob_all = prob_ref[...]
    d_logit = prob_all * (d_gate - jnp.sum(prob_all * d_gate, axis=0, keepdims=True))
    dl_out[...] = d_logit.astype(bf16)
    dl_in[lin] = d_logit.astype(bf16)

    def start_dl(step, carry):
        dl_copy(step).start()
        return carry

    each_other(count, start_dl)
    dw_steps(4)
    for arr, sub in ((0, 2), (1, 2), (1, 3)):
        back_relay(arr, sub)
    dw_steps(4)

    def settle(arr, sub):
        arrive(("left", arr, sub), inbox.at[arr, 0, sub])
        arrive(("right", arr, sub), inbox.at[arr, 1, sub])
        return value(arr, 0, sub) + inbox[arr, 0, sub].astype(f32) + inbox[arr, 1, sub].astype(f32)

    def ship(key, arr, sub, part, val, dst, step):
        rows_at = pl.ds(part * half, half)
        stage[arr, sub - 1, rows_at] = val.astype(bf16)
        back(key, stage.at[arr, sub - 1, rows_at], dst, along_first[arr](step))

    for arr in PAIR:
        val = settle(arr, 1)
        ship(("left2", arr, 1), arr, 1, 1, val[half:], inbox2.at[arr, 0, 1], 1)
        total[arr, 0, :half] = val[:half]
    for arr in PAIR:
        val = settle(arr, 2)
        ship(("far2", arr, 0), arr, 2, 0, val[:half], relay2.at[arr, 0], 1)
        ship(("far2", arr, 1), arr, 2, 1, val[half:], relay2.at[arr, 1], 3)
    for arr in PAIR:
        val = settle(arr, 3)
        ship(("right2", arr, 0), arr, 3, 0, val[:half], inbox2.at[arr, 1, 0], 3)
        total[arr, 0, half:] = val[half:]
    dw_steps(2)
    for arr in PAIR:
        arrive(("far2", arr, 0), relay2.at[arr, 0])
        val = total[arr, 0, :half] + relay2[arr, 0].astype(f32)
        ship(("left2", arr, 0), arr, 1, 0, val, inbox2.at[arr, 0, 0], 1)
        arrive(("far2", arr, 1), relay2.at[arr, 1])
        val = total[arr, 0, half:] + relay2[arr, 1].astype(f32)
        ship(("right2", arr, 1), arr, 3, 1, val, inbox2.at[arr, 1, 1], 3)
    for arr in PAIR:
        total[arr, 1] = settle(arr, 0)

    def wait_dl(step, carry):
        src = lax.rem(lin + step, count)
        landed(dl_in.at[src], dl_recv.at[src])
        return carry

    each_other(count, wait_dl)
    du_router = lax.dot_general(dl_out[...], wr_ref[...], (((0,), (0,)), ((), ())), preferred_element_type=f32)[:tok]
    dwr_out[...] = jnp.zeros_like(dwr_out)

    def dwr_step(idx, carry):
        parts = []
        for pair in range(etp_size):
            low = dl_in[idx * 2 * etp_size + pair].astype(f32)
            high = dl_in[(idx * 2 + 1) * etp_size + pair].astype(f32)
            parts.append((low + pltpu.roll(high, tok, 1)).astype(bf16))
        dwr_out[...] += mm(jnp.concatenate(parts, axis=1), rows[0, idx].reshape(2 * etp_size * tok, d_model))
        return carry

    lax.fori_loop(0, ring, dwr_step, 0)
    dw_steps(len(todo))
    for part in PAIR:
        for arr, base, out in ((0, u_ref, y_out), (1, dy_ref, du_out)):
            arrive(("left2", arr, part), inbox2.at[arr, 0, part])
            arrive(("right2", arr, part), inbox2.at[arr, 1, part])
            rows_at = pl.ds(part * half, half)
            val = base[rows_at].astype(f32) + total[arr, 1, rows_at] + inbox2[arr, 0, part].astype(f32) + inbox2[arr, 1, part].astype(f32)
            if arr == 1:
                val = val + du_router[part * half:(part + 1) * half]
            out[rows_at] = val.astype(bf16)
    for slot in PAIR:
        wait_swaps(slot)
    for copy in pending.values():
        copy.wait()
    for slot, size in enumerate(sends):
        landed(rows.at[0, 0, 0, 0, pl.ds(0, size)], send_sem.at[slot])
    for slot, size in back_sends:
        landed(rows.at[0, 0, 0, 0, pl.ds(0, size)], back_send.at[slot])

    def drain(step, carry):
        gate_copy(step).wait_send()
        dg_copy(step).wait_send()
        dl_copy(step).wait_send()
        return carry

    each_other(count, drain)


def block_call(mesh, u_loc, dy_loc, ids_t, wr_t, w1, w3, w2):
    etp_size, ep_size = mesh.shape["etp"], mesh.shape["ep"]
    tok, d_model = u_loc.shape
    experts, inner = wr_t.shape[0], w1.shape[0]
    count, ring, half = etp_size * ep_size, ep_size // 2, tok // 2
    assert ring == 4 and etp_size == 4
    width = inner // (experts // ep_size)
    vmem = pl.BlockSpec(memory_space=pltpu.VMEM)
    hbm = pl.BlockSpec(memory_space=pl.ANY)
    bf16, f32 = jnp.bfloat16, jnp.float32
    dma = pltpu.SemaphoreType.DMA
    shape = jax.ShapeDtypeStruct
    quad = (2, ring, etp_size)
    return pl.pallas_call(
        functools.partial(block_kernel, etp_size, ring, width),
        out_shape=(shape((tok, d_model), bf16),) * 2 + (shape((experts, d_model), f32),) + (shape((inner, d_model), f32),) * 3 + (shape((3, count * tok, inner), bf16),),
        in_specs=[vmem] * 4 + [hbm] * 3,
        out_specs=(vmem,) * 3 + (hbm,) * 4,
        scratch_shapes=[
            pltpu.VMEM(quad + (2, tok, d_model), bf16),
            pltpu.VMEM((inner, d_model), bf16), pltpu.VMEM((inner, d_model), bf16), pltpu.VMEM((inner, d_model), bf16),
            pltpu.VMEM((3, count * tok, inner), bf16),
            pltpu.VMEM((2, 4, tok, d_model), bf16), pltpu.VMEM((2, 4, tok, d_model), bf16), pltpu.VMEM((3, 4 * tok, inner), bf16), pltpu.VMEM((2, 4 * tok, inner), bf16),
            pltpu.VMEM((ep_size, 8, 128), f32), pltpu.VMEM((count, 8, 128), f32), pltpu.VMEM((count, 8, 128), f32), pltpu.VMEM((experts, 128), f32),
            pltpu.VMEM(quad + (tok, d_model), bf16), pltpu.VMEM(quad + (tok, d_model), bf16),
            pltpu.VMEM((2, 4, tok, d_model), bf16),
            pltpu.VMEM((2, 2, 4, tok, d_model), bf16),
            pltpu.VMEM((2, 2, tok, d_model), f32),
            pltpu.VMEM((2, 3, tok, d_model), bf16),
            pltpu.VMEM((2, 2, half, d_model), bf16),
            pltpu.VMEM((2, 2, 2, half, d_model), bf16),
            pltpu.VMEM((2, 128, d_model), f32),
            pltpu.VMEM((count, 8, 128), f32),
            pltpu.VMEM((count, experts, 128), bf16),
            pltpu.VMEM((experts, 128), bf16),
            dma((3,)), dma((2, 3)), dma((72,)), dma(quad), dma((2, 2)), dma(quad), dma((count,)), dma((count,)),
            dma((2, 2, 2)), dma(quad), dma((48,)), dma((48,)), dma((3,)), dma((2,)), dma((count,)), dma((count,)), dma((count,)), dma((count,)),
        ],
        compiler_params=pltpu.CompilerParams(collective_id=0, has_side_effects=True, vmem_limit_bytes=67043328),
        name="moe_block",
    )(u_loc, dy_loc, ids_t, wr_t, w1, w3, w2)[:6]


def solution(mesh):
    tok_spec = P(("dp", "ep", "etp"), None)
    col_spec = P("ep", None, "etp")
    row_spec = P("ep", "etp", None)
    in_specs = (tok_spec, tok_spec, tok_spec, P(None, None), col_spec, col_spec, row_spec)
    out_specs = (tok_spec, tok_spec, P(("dp", "ep"), None, "etp"), P(("dp", "ep"), None, "etp"), P(("dp", "ep"), "etp", None), P("dp", None))

    def device_step(u_loc, dy_loc, ids_loc, w_router, w_gate, w_up, w_down):
        local_exp, d_model, width = w_gate.shape
        inner = local_exp * width
        w1 = jnp.swapaxes(w_gate, 1, 2).reshape(inner, d_model)
        w3 = jnp.swapaxes(w_up, 1, 2).reshape(inner, d_model)
        w2 = w_down.reshape(inner, d_model)
        y_loc, du_loc, dwr_t, dw1, dw3, dw2 = block_call(mesh, u_loc, dy_loc, ids_loc.T, w_router.T, w1, w3, w2)
        unfold = lambda d: jnp.swapaxes(d.reshape(local_exp, width, d_model), 1, 2)
        return y_loc, du_loc, unfold(dw1), unfold(dw3), dw2.reshape(local_exp, width, d_model), dwr_t.T

    return jax.shard_map(device_step, mesh=mesh, in_specs=in_specs, out_specs=out_specs, check_vma=False)
```

time: 500 us -> 124 us (0.25)
  waiting for transfers between devices: 357 us -> 0 us
  Pallas kernels: 0 us -> 109 us
  matrix products: 84.5 us -> 0 us
  blocking collectives: 33.3 us -> 0 us
  between operations: 14.4 us -> 0.65 us
  local copies, waits for them, and re-layouts: 4.39 us -> 14.6 us
  other arithmetic: 5.7 us -> 0.01 us
    reduce_scatter x2 -> x0, waiting for transfers between devices: 195 us -> none  [the longest x1 97.8 us: device_step(): du_own = lax.psum_scatter(du_part, axes, scatter_dimension=0, tiled=True)]
    pallas_call x0 -> x1, Pallas kernels: none -> 109 us  [block_call(): pl.pallas_call(functools.partial(block_kernel, etp_size, ring, width), ou...]
    psum x1 -> x0, waiting for transfers between devices: 95.7 us -> none  [device_step(): dw_router = lax.psum(dot_f32(u_loc, d_logit.astype(jnp.bfloat16), tn), axes)]
    dot_general x12 -> x0, matrix products: 84.5 us -> none  [the longest x11 83.4 us: dot_f32(): lax.dot_general(lhs, rhs, (contract, ((), ())), preferred_element_type=jn...]
    all_gather x2 -> x0, waiting for transfers between devices: 49.6 us -> none  [the longest x1 35.7 us: device_step(): dy_all = lax.all_gather(dy_loc, axes, axis=0, tiled=True)]
    all_gather x1 -> x0, blocking collectives: 33.3 us -> none  [device_step(): gate_all = lax.all_gather(gate_loc, axes, axis=0, tiled=True)]
    unnamed x7 -> x0, waiting for transfers between devices: 16.6 us -> none
    unnamed x30 -> x14, local copies, waits for them, and re-layouts: 4.03 us -> 14.6 us
  transfers between devices with their start and end apart: 6 -> 0, of which waited for: 6 -> 0; matrix products, arithmetic and copies ran while one was open for 14% -> 0% of each run, Pallas kernels for 0% -> 0%
where the time goes in v4:
time: 124 us
  Pallas kernels  109 us (88%)
  local copies, waits for them, and re-layouts  14.6 us (12%)
    pallas_call x1, Pallas kernels, block_call(): pl.pallas_call(functools.partial(block_kernel, etp_size, ring, width), ou...  109 us
    unnamed x14, local copies, waits for them, and re-layouts  14.6 us

profile of v4, /device:TPU:97, one launch (start us, length us, event | category | flops | bytes accessed | tf_op | source)
XLA Modules:
  0.0 124.1 jit_solution(12489020639871292091)
XLA Ops:
  0.6 108.8 %moe_block.1 = (bf16[64,1536]{1,0:T(8,128)(2,1)}, bf16[64,1536]{1,0:T(8,128)(2,1)}, f32[32,1536]{1,0:T(8,128)}, f32[768,1536]{1,0:T(8,128)}, f32[768,1536]{1,0:T...) custom-call(bf16[64,1536]{1,0:T(8,128)(2,1)} %u_ref.1, bf16[64,1536]{1,0:T(8,128)(2,1)} %dy_ref.1, ...), custom_call_target="tpu_custom_call" | custom-call | tf_op jit(solution)/shard_map/moe_block/pallas_call | solution.py:562
  109.5 1.6 %copy.19 = bf16[64,1536]{1,0:T(8,128)(2,1)} copy(bf16[64,1536]{1,0:T(8,128)(2,1)} %get-tuple-element.24) | data formatting | bytes 393216
  111.1 1.6 %copy.20 = bf16[64,1536]{1,0:T(8,128)(2,1)} copy(bf16[64,1536]{1,0:T(8,128)(2,1)} %get-tuple-element.25) | data formatting | bytes 393216
  112.7 0.0 copy-start
  112.7 0.0 slice-start
  112.7 5.2 %copy.21 = f32[4,1536,192]{1,2,0:T(8,128)} copy(f32[4,1536,192]{1,2,0:T(8,128)} %bitcast.21) | data formatting | bytes 9437184
  117.9 0.0 copy-done
  117.9 0.0 slice-start.1
  117.9 2.4 %copy.22 = f32[4,1536,192]{1,2,0:T(8,128)} copy(f32[4,1536,192]{1,2,0:T(8,128)S(1)} %bitcast.20) | data formatting | bytes 9437184
  120.3 0.4 slice-done
  120.7 0.6 slice-done.1
  121.2 0.0 copy-start.1
  121.2 2.2 %copy.23 = f32[4,192,1536]{2,1,0:T(8,128)} copy(f32[4,192,1536]{2,1,0:T(8,128)S(1)} %bitcast.19) | data formatting | bytes 9437184
  123.4 0.0 copy-done.1
  123.4 0.7 copy.24
  (1 shorter events, 0.0 us)
Async XLA Ops:
  112.7 5.2 %copy-start = (f32[768,1536]{1,0:T(8,128)S(1)}, f32[768,1536]{1,0:T(8,128)}, u32[]{:S(2)}) copy-start(f32[768,1536]{1,0:T(8,128)} %get-tuple-element.15) | copy-start | bytes 14155780
  112.7 8.0 %slice-start = ((s8[4718592]{0:T(1024)(128)(4,1)}), s8[4194304]{0:T(1024)(128)(4,1)S(1)}, s32[]{:S(2)}) async-start(s8[4718592]{0:T(1024)(128)(4,1)} %bitcast.17), calls=%async_computation | async-start | bytes 8388608
  117.9 3.3 %slice-start.1 = ((s8[4718592]{0:T(1024)(128)(4,1)}), s8[524288]{0:T(1024)(128)(4,1)S(1)}, s32[]{:S(2)}) async-start(s8[4718592]{0:T(1024)(128)(4,1)} %bitcast.17), calls=%async_computation.1 | async-start | bytes 1048576
  121.2 2.2 %copy-start.1 = (f32[32,1536]{1,0:T(8,128)S(1)}, f32[32,1536]{1,0:T(8,128)}, u32[]{:S(2)}) copy-start(f32[32,1536]{1,0:T(8,128)} %get-tuple-element.17) | copy-start | bytes 589828

commit v5 on v4

--- a/solution.py
+++ b/solution.py
@@ -162,11 +162,11 @@
         gate_copy(step).start()
         return carry
 
+
+    first_own(0)
+    first_own(1)
     each_other(count, start_gate)
     gate_in[lin] = gate_out[ep]
-
-    first_own(0)
-    first_own(1)
     second_own(1)
     second_own(0)
     for arr, ref in enumerate((u_ref, dy_ref)):
@@ -434,9 +434,11 @@
     back_far(1, 2)
     back_far(1, 3)
     back_direct(0, 2)
+    for arr, sub in ((0, 0), (1, 0), (0, 3)):
+        back_relay(arr, sub)
     dw_steps(2)
-    for arr, sub in ((0, 0), (1, 0), (0, 3), (0, 1), (1, 1)):
-        back_relay(arr, sub)
+    for arr in PAIR:
+        back_relay(arr, 1)
 
     def wait_dg(step, carry):
         src = lax.rem(lin + step, count)
@@ -589,6 +591,38 @@
     )(u_loc, dy_loc, ids_t, wr_t, w1, w3, w2)[:6]
 
 
+def copy_kernel(number, *refs):
+    srcs, dsts, bufs = refs[:number], refs[number:2 * number], refs[2 * number:3 * number]
+    in_sem, out_sem = refs[3 * number:]
+    loads, stores = [], []
+    for src, dst, buf in zip(srcs, dsts, bufs):
+        step = min(src.shape[0], 256)
+        for start in range(0, src.shape[0], step):
+            at = pl.ds(start, step)
+            loads.append(pltpu.make_async_copy(src.at[at], buf.at[at], in_sem.at[len(loads)]))
+            stores.append(pltpu.make_async_copy(buf.at[at], dst.at[at], out_sem.at[len(stores)]))
+    for copy in loads:
+        copy.start()
+    for load, store in zip(loads, stores):
+        load.wait()
+        store.start()
+    for copy in stores:
+        copy.wait()
+
+
+def copy_call(arrays):
+    hbm = pl.BlockSpec(memory_space=pltpu.HBM)
+    return pl.pallas_call(
+        functools.partial(copy_kernel, len(arrays)),
+        out_shape=tuple(jax.ShapeDtypeStruct(a.shape, a.dtype) for a in arrays),
+        in_specs=[hbm] * len(arrays),
+        out_specs=(hbm,) * len(arrays),
+        scratch_shapes=[pltpu.VMEM(a.shape, a.dtype) for a in arrays] + [pltpu.SemaphoreType.DMA((16,)), pltpu.SemaphoreType.DMA((16,))],
+        compiler_params=pltpu.CompilerParams(vmem_limit_bytes=67043328),
+        name="place_results",
+    )(*arrays)
+
+
 def solution(mesh):
     tok_spec = P(("dp", "ep", "etp"), None)
     col_spec = P("ep", None, "etp")
@@ -602,7 +636,7 @@
         w1 = jnp.swapaxes(w_gate, 1, 2).reshape(inner, d_model)
         w3 = jnp.swapaxes(w_up, 1, 2).reshape(inner, d_model)
         w2 = w_down.reshape(inner, d_model)
-        y_loc, du_loc, dwr_t, dw1, dw3, dw2 = block_call(mesh, u_loc, dy_loc, ids_loc.T, w_router.T, w1, w3, w2)
+        y_loc, du_loc, dwr_t, dw1, dw3, dw2 = copy_call(block_call(mesh, u_loc, dy_loc, ids_loc.T, w_router.T, w1, w3, w2))
         unfold = lambda d: jnp.swapaxes(d.reshape(local_exp, width, d_model), 1, 2)
         return y_loc, du_loc, unfold(dw1), unfold(dw3), dw2.reshape(local_exp, width, d_model), dwr_t.T
 

time: 124 us -> 121 us (0.976)
  local copies, waits for them, and re-layouts: 14.6 us -> 0 us
  Pallas kernels: 109 us -> 120 us
    unnamed x14 -> x0, local copies, waits for them, and re-layouts: 14.6 us -> none
    pallas_call x0 -> x1, Pallas kernels: none -> 11 us  [copy_call(): pl.pallas_call(functools.partial(copy_kernel, len(arrays)), out_shape=tup...]
where the time goes in v5:
time: 121 us
  Pallas kernels  120 us (99%)
    pallas_call x1, Pallas kernels, block_call(): pl.pallas_call(functools.partial(block_kernel, etp_size, ring, width), ou...  109 us
    pallas_call x1, Pallas kernels, copy_call(): pl.pallas_call(functools.partial(copy_kernel, len(arrays)), out_shape=tup...  11 us

profile of v5, /device:TPU:97, one launch (start us, length us, event | category | flops | bytes accessed | tf_op | source)
XLA Modules:
  0.0 120.8 jit_solution(4325215415845882741)
XLA Ops:
  0.6 109.0 %moe_block.1 = (bf16[64,1536]{1,0:T(8,128)(2,1)}, bf16[64,1536]{1,0:T(8,128)(2,1)}, f32[32,1536]{1,0:T(8,128)}, f32[768,1536]{1,0:T(8,128)}, f32[768,1536]{1,0:T...) custom-call(bf16[64,1536]{1,0:T(8,128)(2,1)} %u_ref.1, bf16[64,1536]{1,0:T(8,128)(2,1)} %dy_ref.1, ...), custom_call_target="tpu_custom_call" | custom-call | tf_op jit(solution)/shard_map/moe_block/pallas_call | solution.py:564
  109.7 11.0 %place_results.1 = (bf16[64,1536]{1,0:T(8,128)(2,1)}, bf16[64,1536]{1,0:T(8,128)(2,1)}, f32[32,1536]{1,0:T(8,128)}, f32[768,1536]{1,0:T(8,128)}, f32[768,1536]{1,0:T(8,128)}, /*index=5*/f32[768,1536]{1,0:T(8,128)}) custom-call(bf16[64,1536]{1,0:T(8,128)(2,1)} %get-tuple-element.18.refs_0_, bf16[64,1536]{1,0:T(8,128)(2,1)} %get-tuple-element.19.refs_1_, ...), custom_call_target="tpu_custom_call" | custom-call | tf_op jit(solution)/shard_map/place_results/pallas_call | solution.py:615
